TPU v7x, 256 devices: a whole 4x4x8 slice. The times are simulated.
256 devices in a mesh: gx: 8 (over z_lo, x), gy: 4 (over z_hi), gz: 8 (over y, core).
Axes of the slice: x: 4, y: 4, z: 8 (z_hi: 4, z_lo: 2; z = z_hi * 2 + z_lo), core: 2. Of those that a mesh axis runs over, the one named last changes fastest.
Arguments:
- displacement: bfloat16 [3, 32, 128, 128], P(None, 'gx', 'gy', 'gz'), may hold values from -6 to 6
- lift_weight: bfloat16 [27, 64, 3], replicated, may hold values from -1 to 1
- encode_weight: bfloat16 [27, 64, 64], replicated, may hold values from -0.21875 to 0.21875
- downward_weight: bfloat16 [8, 128, 64], replicated, may hold values from -0.375 to 0.375
- middle_first: bfloat16 [27, 128, 128], replicated, may hold values from -0.15625 to 0.15625
- middle_second: bfloat16 [27, 128, 128], replicated, may hold values from -0.15625 to 0.15625
- up_weight: bfloat16 [8, 64, 128], replicated, may hold values from -0.75 to 0.75
- decode_weight: bfloat16 [27, 64, 128], replicated, may hold values from -0.15625 to 0.15625
- head_weight: bfloat16 [3, 64], replicated, may hold values from -1 to 1
Outputs:
- imitated: float32 [3, 32, 128, 128], P(None, 'gx', 'gy', 'gz')
All inputs are finite; a program needn't handle non-finite values.
Results may differ from a plain program's by a relative error of at most 0.0055.
Values may be sent and summed in bfloat16 or wider, within the bound.
No kernel may reach another device: no remote copies, remote signals or barrier semaphores. Data moves between devices by JAX's collectives and lax.ppermute only.
A program may use at most 64 MiB of HBM per device.

v0:
```python
import jax
import jax.numpy as jnp
import numpy as np
from jax import lax
from jax.experimental import pallas as pl
from jax.experimental.pallas import tpu as pltpu
from jax.sharding import PartitionSpec as P

BF, F32 = jnp.bfloat16, jnp.float32


def shift(block, axis, step):
    count = lax.axis_size(axis)
    return lax.ppermute(block, axis, [(i, (i + step) % count) for i in range(count)])


def act(value):
    return jnp.maximum(value, 0.1 * value)


def picker():
    table = np.zeros((3, 128, 8, 128), np.float32)
    for b in range(3):
        for q in range(8):
            for a in range(2):
                for ch in range(3):
                    for zi in range(6):
                        z = 4 * q + zi - 1
                        if 0 <= z < 32:
                            row = 48 + 8 * ch + z if z < 8 else 16 * ch + z - 8 if z < 24 else 48 + 8 * ch + z
                            table[b, row, q, 18 * (3 * a + b) + 6 * ch + zi] = 1
    return table.reshape(384, 1024)


def lift_matrix(w):
    w = jnp.transpose(w.reshape(9, 3, 64, 3), (0, 3, 1, 2))
    cols = [jnp.pad(w, ((0, 0), (0, 0), (zo, 3 - zo), (0, 0))) for zo in range(4)]
    m = jnp.concatenate(cols, axis=3).reshape(162, 256)
    return jnp.concatenate([m[:108], jnp.zeros((20, 256), BF), m[108:], jnp.zeros((74, 256), BF)], axis=0)


def quad_matrix(w):
    t = jnp.swapaxes(w, 1, 2).reshape(9, 3, w.shape[2], 64)
    c0, c1, c2 = t[:, 0], t[:, 1], t[:, 2]
    o = jnp.zeros_like(c0)
    cols = [[c1, c2, o, o, o, c0], [c0, c1, c2, o, o, o], [o, c0, c1, c2, o, o], [o, o, c0, c1, c2, o]]
    return jnp.concatenate([jnp.concatenate(c, axis=1) for c in cols], axis=2)


def pair_matrix(w):
    t = jnp.swapaxes(w, 1, 2).reshape(9, 3, 128, 128)
    c0, c1, c2 = t[:, 0], t[:, 1], t[:, 2]
    o = jnp.zeros_like(c0)
    cols = [[c0, c1, c2, o], [o, c0, c1, c2]]
    return jnp.concatenate([jnp.concatenate(c, axis=1) for c in cols], axis=2)


def head_matrix(w):
    wt = w.T
    m = jnp.einsum("zs,ck->zcks", jnp.eye(16, dtype=BF), wt)
    return jnp.pad(m.reshape(1024, 48), ((0, 0), (0, 80)))


def weights(lift, encode, down, m1, m2, up, decode, head):
    we = quad_matrix(encode).reshape(3456, 256)
    ws, wu = quad_matrix(decode[:, :, :64]), quad_matrix(decode[:, :, 64:])
    wdec = jnp.concatenate([ws, wu], axis=1).reshape(6912, 256)
    return (
        lift_matrix(lift), we, jnp.swapaxes(down, 1, 2).reshape(512, 128),
        pair_matrix(m1).reshape(4608, 256), pair_matrix(m2).reshape(4608, 256),
        jnp.transpose(up, (2, 0, 1)).reshape(128, 512), wdec, head_matrix(head),
    )


def dot(a, b):
    return jnp.dot(a, b, preferred_element_type=F32)


def rows(parts):
    flat = [p.reshape(-1, p.shape[-1]) for p in parts]
    return flat[0] if len(flat) == 1 else jnp.concatenate(flat, axis=1)


def up_one(v):
    return pltpu.roll(v, v.shape[-2] - 1, v.ndim - 2)


def kernel(d_ref, s_ref, wl_ref, we_ref, wd_ref, w1_ref, w2_ref, wu_ref, wdec_ref, wh_ref, o_ref,
           dt, db, fp, fe, sk, sd, c1, c2, de, uu, es, eu):
    for yo in range(8):
        for xo in range(12):
            t = [d_ref[pl.ds((8 * xi + xo) * 48 + yo, 8, stride=6), :] for xi in range(2)]
            dt[yo, xo] = jnp.concatenate(t, axis=0).astype(BF)

    lane = lax.broadcasted_iota(jnp.int32, (16, 128), 1)
    first_slots = lane < 54
    low = lane < 64

    for h in range(4):
        r = dot(rows([dt[b:b + 6] for b in range(3)]), s_ref[:, 256 * h:256 * h + 256])
        r = r.astype(BF).reshape(6, 12, 16, 256)
        db[2 * h] = r[..., :128]
        db[2 * h + 1] = r[..., 128:]

    def lift_step(q, carry):
        for g in range(2):
            y = slice(3 * g, 3 * g + 3)
            ta = jnp.where(first_slots, db[q, y, 0:10], db[q, y, 1:11])
            r = act(dot(rows([ta, db[q, y, 2:12]]), wl_ref[...]))
            for half in range(2):
                part = r[:, 128 * half:128 * half + 128].reshape(3, 10, 16, 128)
                fp[2 * q + half, y] = part.astype(BF)
                if g == 0:
                    low_rows = part[0:2].reshape(40, 8, 128)
                    fp[2 * q + half, 6:8] = up_one(low_rows).reshape(2, 10, 16, 128).astype(BF)
        return carry

    lax.fori_loop(0, 8, lift_step, 0)

    def edge_step(q, carry):
        fe[q] = jnp.where(low, fp[2 * q + 3], fp[2 * q])
        return carry

    lax.fori_loop(0, 7, edge_step, 0)

    def encode_step(q, carry):
        for g in range(2):
            y0 = 3 * g
            acc = None
            for lo, hi in ((0, 2), (2, 4), (4, 6), (6, 9)):
                parts = []
                for t in range(lo, hi):
                    a, b = t // 3, t % 3
                    sl = (slice(y0 + b, y0 + b + 3), slice(a, a + 8))
                    parts += [fp[(2 * q + 1,) + sl], fp[(2 * q + 2,) + sl], fe[(q,) + sl]]
                p = dot(rows(parts), we_ref[384 * lo:384 * hi, :])
                acc = p if acc is None else acc + p
            r = act(acc).reshape(3, 8, 2, 8, 256)
            for half in range(2):
                part = r[..., 128 * half:128 * half + 128]
                packed = part.reshape(3, 8, 16, 128).astype(BF)
                sp = 2 * q + half
                for yy in range(3):
                    yo = y0 + yy
                    sk[sp, yo // 2, yo % 2] = packed[yy].reshape(4, 2, 16, 128)
                    mixed = [jnp.concatenate([part[yy, 5 + xo, 0] if 5 + xo < 8 else part[yy, 5 + xo - 8, 1],
                                              part[yy, 7 + xo, 0] if 7 + xo < 8 else part[yy, 7 + xo - 8, 1]], axis=0)
                             for xo in range(4)]
                    mixed = jnp.stack(mixed).reshape(8, 8, 128)
                    if yo == 5:
                        sd[sp, 0] = mixed.reshape(4, 16, 128).astype(BF)
                    moved = up_one(mixed)
                    sd[sp, yo + 1] = moved.reshape(4, 16, 128).astype(BF)
                    if yo == 0:
                        sd[sp, 7] = up_one(moved).reshape(4, 16, 128).astype(BF)
        return carry

    lax.fori_loop(0, 7, encode_step, 0)

    r = act(dot(rows([sk[:, :, b, :, a] for a in range(2) for b in range(2)]), wd_ref[...]))
    r = r.reshape(7, 2, 3, 4, 2, 8, 128)
    for yo in range(3):
        for xo in range(5):
            t = jnp.stack([r[:, :, yo, xo % 4, xo // 4], r[:, :, yo, (3 + xo) % 4, (3 + xo) // 4]], axis=2)
            c1[:, :, yo, xo] = t.reshape(7, 2, 16, 128).astype(BF)
            if yo < 2:
                c1[:, :, yo + 3, xo] = up_one(t.reshape(28, 8, 128)).reshape(7, 2, 16, 128).astype(BF)

    def middle(src, w_ref, zp, xn):
        acc = None
        for t in range(9):
            a, b = t // 3, t % 3
            parts = [src[zi // 2:zi // 2 + zp, zi % 2, b:b + 3, a:a + xn] for zi in range(4)]
            p = dot(rows(parts), w_ref[512 * t:512 * t + 512, :])
            acc = p if acc is None else acc + p
        return act(acc).reshape(zp, 3, xn, 2, 8, 256)

    r = middle(c1, w1_ref, 6, 3)
    for half in range(2):
        part = r[..., 128 * half:128 * half + 128]
        for yo in range(3):
            for xo in range(4):
                t = jnp.stack([part[:, yo, xo % 3, xo // 3], part[:, yo, (2 + xo) % 3, (2 + xo) // 3]], axis=1)
                c2[:, half, yo, xo] = t.reshape(6, 16, 128).astype(BF)
                if yo < 2:
                    c2[:, half, yo + 3, xo] = up_one(t.reshape(12, 8, 128)).reshape(6, 16, 128).astype(BF)

    r = middle(c2, w2_ref, 5, 2).reshape(5, 3, 2, 16, 256).astype(BF)
    de[:, 0] = r[..., :128]
    de[:, 1] = r[..., 128:]

    r = act(dot(rows([de[...]]), wu_ref[...])).reshape(5, 2, 3, 2, 2, 8, 512)
    for yo in range(6):
        b = yo % 2
        for xo in range(4):
            t = []
            for f in (1 + xo, 3 + xo):
                a = f % 2
                n = 128 * (2 * a + b)
                t.append(r[:, :, yo // 2, (f // 2) % 2, f // 4, :, n:n + 128])
            t = jnp.stack(t, axis=2)
            if yo > 0:
                uu[:, :, yo - 1, xo] = t.reshape(5, 2, 16, 128).astype(BF)
            if yo < 3:
                uu[:, :, yo + 5, xo] = up_one(t.reshape(20, 8, 128)).reshape(5, 2, 16, 128).astype(BF)

    for q in range(4):
        es[q] = jnp.where(low, sd[2 * q + 5], sd[2 * q + 2])
        eu[q] = jnp.where(low, uu[q + 1, 1], uu[q, 0])

    for g in range(1):
        acc = None
        for t in range(9):
            a, b = t // 3, t % 3
            ys, xs = slice(b, b + 6), slice(a, a + 2)
            own = [jnp.stack([sd[2 * q + 3 + k, ys, xs] for q in range(4)]) for k in range(2)]
            parts = own + [es[:, ys, xs], uu[0:4, 1, ys, xs], uu[1:5, 0, ys, xs], eu[:, ys, xs]]
            p = dot(rows(parts), wdec_ref[768 * t:768 * t + 768, :])
            acc = p if acc is None else acc + p
        j = act(acc).astype(BF).reshape(4, 192, 256)
        o_ref[...] = dot(jnp.concatenate([j[q] for q in range(4)], axis=1), wh_ref[...])


def compute(d, ws):
    flat = jnp.pad(d.astype(F32).reshape(960, 96), ((0, 8), (0, 32)))
    V = pltpu.VMEM
    out = pl.pallas_call(
        kernel,
        out_shape=jax.ShapeDtypeStruct((192, 128), F32),
        in_specs=[pl.BlockSpec(memory_space=pltpu.VMEM)] * 10,
        out_specs=pl.BlockSpec(memory_space=pltpu.VMEM),
        scratch_shapes=[
            V((8, 12, 16, 128), BF), V((8, 6, 12, 16, 128), BF), V((16, 8, 10, 16, 128), BF), V((7, 8, 10, 16, 128), BF),
            V((14, 3, 2, 4, 2, 16, 128), BF), V((14, 8, 4, 16, 128), BF), V((7, 2, 5, 5, 16, 128), BF),
            V((6, 2, 5, 4, 16, 128), BF), V((5, 2, 3, 2, 16, 128), BF), V((5, 2, 8, 4, 16, 128), BF),
            V((4, 8, 4, 16, 128), BF), V((4, 8, 4, 16, 128), BF),
        ],
        compiler_params=pltpu.CompilerParams(vmem_limit_bytes=60 << 20),
        cost_estimate=pl.CostEstimate(flops=20_000_000_000, bytes_accessed=20_000_000, transcendentals=0),
    )(flat, jnp.asarray(picker(), BF), *ws)
    out = out[:, :48].reshape(6, 2, 2, 8, 3, 16)
    return jnp.transpose(out, (4, 2, 1, 3, 0, 5)).reshape(3, 4, 48, 16)[:, :, :32]


def local(displacement, *raw):
    ws = weights(*raw)
    d = jnp.concatenate([displacement[0], displacement[1], displacement[2]], axis=-1)
    d = jnp.concatenate([shift(d, "gx", 2), shift(d, "gx", 1), d, shift(d, "gx", -1), shift(d, "gx", -2)], axis=0)
    d = jnp.concatenate([shift(d[:, 24:], "gy", 1), d, shift(d[:, :8], "gy", -1)], axis=1)
    left = jnp.concatenate([d[..., 16 * k + 8:16 * k + 16] for k in range(3)], axis=-1)
    right = jnp.concatenate([d[..., 16 * k:16 * k + 8] for k in range(3)], axis=-1)
    d = jnp.concatenate([d, shift(left, "gz", 1), shift(right, "gz", -1)], axis=-1)
    return displacement.astype(F32) + compute(d, ws)


def solution(mesh):
    placed = (P(None, "gx", "gy", "gz"), P(), P(), P(), P(), P(), P(), P(), P())
    return jax.shard_map(local, mesh=mesh, in_specs=placed, out_specs=P(None, "gx", "gy", "gz"), check_vma=False)
```

profile of v0, /device:TPU:2, one launch (start us, length us, event | category | flops | bytes accessed | tf_op | source)
XLA Modules:
  0.0 131.4 jit_solution(1092882616949724265)
XLA Ops:
  1.4 2.1 %collective-permute-start = (bf16[4,32,48]{1,2,0:T(8,128)(2,1)}, bf16[4,32,48]{1,2,0:T(8,128)(2,1)}, u32[]{:S(2)}, u32[]{:S(2)}) collective-permute-start(bf16[4,32,48]{1,2,0:T(8,128)(2,1)} %pad_maximum_fusion.8), channel_id=1, source_target_pairs={{0,64},{32,96},{64,128},{96,160},{128,192},{160,224},{192,0},{224,... | collective-permute-start | bytes 36872 | tf_op jit(solution)/shard_map/ppermute | solution.py:14
  3.5 1.2 collective-permute-start.1
  5.6 2.5 %collective-permute-start.3 = (bf16[4,32,48]{1,2,0:T(8,128)(2,1)}, bf16[4,32,48]{1,2,0:T(8,128)(2,1)}, u32[]{:S(2)}, u32[]{:S(2)}) collective-permute-start(bf16[4,32,48]{1,2,0:T(8,128)(2,1)} %pad_maximum_fusion.8), channel_id=1, source_target_pairs={{0,192},{32,224},{64,0},{96,32},{128,64},{160,96},{192,128},{224,1... | collective-permute-start | bytes 36872 | tf_op jit(solution)/shard_map/ppermute | solution.py:14
  10.8 1.4 %fusion.29 = (bf16[27,64,64]{2,1,0:T(8,128)(2,1)S(1)}, bf16[27,64,64]{2,1,0:T(8,128)(2,1)S(1)}) fusion(bf16[27,64,128]{2,1,0:T(8,128)(2,1)} %param.17), kind=kLoop, calls=%fused_computation.90 | loop fusion | bytes 884736 | tf_op jit(solution)/shard_map/slice | solution.py:66
  14.0 1.1 copy.89
  15.1 1.1 copy.90
  17.0 1.7 %copy.94 = bf16[9,1,64,64]{3,2,0,1:T(8,128)(2,1)} copy(bf16[9,1,64,64]{2,3,1,0:T(8,128)(2,1)} %get-tuple-element.18) | data formatting | bytes 147456
  18.7 1.7 %copy.92 = bf16[9,1,64,64]{3,2,0,1:T(8,128)(2,1)} copy(bf16[9,1,64,64]{2,3,1,0:T(8,128)(2,1)} %get-tuple-element.17) | data formatting | bytes 147456
  20.3 1.7 %copy.93 = bf16[9,1,64,64]{3,2,0,1:T(8,128)(2,1)} copy(bf16[9,1,64,64]{2,3,1,0:T(8,128)(2,1)} %get-tuple-element.16) | data formatting | bytes 147456
  22.0 1.8 %fusion.31 = (bf16[9,1,64,64]{2,3,1,0:T(8,128)(2,1)}, bf16[9,1,64,64]{2,3,1,0:T(8,128)(2,1)S(1)}, bf16[9,1,64,64]{2,3,1,0:T(8,128)(2,1)S(1)}) fusion(bf16[9,3,64,64]{2,3,1,0:T(8,128)(2,1)} %bitcast.110), kind=kLoop, calls=%fused_computation.92 | loop fusion | bytes 442368 | tf_op jit(solution)/shard_map/slice | solution.py:44
  24.1 1.1 copy.81
  28.2 2.1 %fusion.27 = (bf16[9,1,128,128]{2,3,1,0:T(8,128)(2,1)}, bf16[9,1,128,128]{2,3,1,0:T(8,128)(2,1)}, bf16[9,1,128,128]{2,3,1,0:T(8,128)(2,1)}) fusion(bf16[9,3,128,128]{2,3,1,0:T(8,128)(2,1)} %bitcast.107), kind=kLoop, calls=%fused_computation.88 | loop fusion | bytes 1769472 | tf_op jit(solution)/shard_map/slice | solution.py:52
  30.2 1.9 %copy.83 = bf16[9,1,128,128]{3,2,0,1:T(8,128)(2,1)} copy(bf16[9,1,128,128]{2,3,1,0:T(8,128)(2,1)} %get-tuple-element.8) | data formatting | bytes 589824
  32.1 1.8 %copy.84 = bf16[9,1,128,128]{3,2,0,1:T(8,128)(2,1)} copy(bf16[9,1,128,128]{2,3,1,0:T(8,128)(2,1)} %get-tuple-element.9) | data formatting | bytes 589824
  33.9 1.8 %copy.85 = bf16[9,1,128,128]{3,2,0,1:T(8,128)(2,1)} copy(bf16[9,1,128,128]{2,3,1,0:T(8,128)(2,1)} %get-tuple-element.10) | data formatting | bytes 589824
  35.8 2.1 %fusion.26 = (bf16[9,1,128,128]{2,3,1,0:T(8,128)(2,1)}, bf16[9,1,128,128]{2,3,1,0:T(8,128)(2,1)}, bf16[9,1,128,128]{2,3,1,0:T(8,128)(2,1)}) fusion(bf16[9,3,128,128]{2,3,1,0:T(8,128)(2,1)} %bitcast.108), kind=kLoop, calls=%fused_computation.87 | loop fusion | bytes 1769472 | tf_op jit(solution)/shard_map/slice | solution.py:52
  37.9 1.8 %copy.86 = bf16[9,1,128,128]{3,2,0,1:T(8,128)(2,1)} copy(bf16[9,1,128,128]{2,3,1,0:T(8,128)(2,1)} %get-tuple-element.5) | data formatting | bytes 589824
  39.7 1.9 %copy.87 = bf16[9,1,128,128]{3,2,0,1:T(8,128)(2,1)} copy(bf16[9,1,128,128]{2,3,1,0:T(8,128)(2,1)} %get-tuple-element.6) | data formatting | bytes 589824
  41.6 1.9 %copy.88 = bf16[9,1,128,128]{3,2,0,1:T(8,128)(2,1)} copy(bf16[9,1,128,128]{2,3,1,0:T(8,128)(2,1)} %get-tuple-element.7) | data formatting | bytes 589824
  45.7 1.6 %constant_dynamic-update-slice_fusion.23 = (bf16[9,384,64]{2,1,0:T(8,128)(2,1)}, bf16[9,384,64]{2,1,0:T(8,128)(2,1)S(1)}) fusion(bf16[9,384,64]{2,1,0:T(8,128)(2,1)} %constant_dynamic-update-slice_fusion.24, bf16[9,1,64,64]{3,2,0,1:T(8,128)(2,1)} %copy.94, bf16[9,384,64]{2,1,0:T(8,128)(2,1)S(1)} %broadcast_dynamic-update-slice_fusion), kind=kLoop, calls=%fused_computation.74 | loop fusion | bytes 442368
  47.3 1.8 %constant_dynamic-update-slice_fusion.22 = (bf16[9,384,64]{2,1,0:T(8,128)(2,1)}, bf16[9,384,64]{2,1,0:T(8,128)(2,1)S(1)}) fusion(bf16[9,384,64]{2,1,0:T(8,128)(2,1)} %get-tuple-element.42, bf16[9,1,64,64]{3,2,0,1:T(8,128)(2,1)} %copy.92, bf16[9,384,64]{2,1,0:T(8,128)(2,1)S(1)} %get-tuple-element.43), kind=kLoop, calls=%fused_computation.73 | loop fusion | bytes 442368
  49.1 1.6 %constant_dynamic-update-slice_fusion.21 = (bf16[9,384,64]{2,1,0:T(8,128)(2,1)}, bf16[9,384,64]{2,1,0:T(8,128)(2,1)S(1)}) fusion(bf16[9,384,64]{2,1,0:T(8,128)(2,1)} %get-tuple-element.40, bf16[9,1,64,64]{3,2,0,1:T(8,128)(2,1)} %copy.93, bf16[9,384,64]{2,1,0:T(8,128)(2,1)S(1)} %get-tuple-element.41), kind=kLoop, calls=%fused_computation.72 | loop fusion | bytes 442368
  51.9 4.1 %pad_maximum_fusion.4 = bf16[9,384,256]{2,1,0:T(8,128)(2,1)} fusion(bf16[9,384,64]{2,1,0:T(8,128)(2,1)S(1)} %constant_dynamic-update-slice_fusion.9, bf16[9,384,64]{2,1,0:T(8,128)(2,1)S(1)} %copy-done.5, bf16[9,192,64]{2,1,0:T(8,128)(2,1)S(1)} %broadcast.26, bf16[9,64,64]{2,1,0:T(8,128)(2,1)S(1)} %bitcast.91, bf16[9,64,64]{2,1,0:T(8,128)(2,1)S(1)} %bitcast.90, ...), kind=kLoop, calls=%fused_computation.11 | loop fusion | flops 17694720 | bytes 3096576 | tf_op jit(solution)/shard_map/concatenate | solution.py:47
  56.1 2.7 %fusion.1 = (bf16[9,512,256]{2,1,0:T(8,128)(2,1)}, bf16[9,512,256]{2,1,0:T(8,128)(2,1)}) fusion(bf16[9,128,128]{2,1,0:T(8,128)(2,1)S(1)} %broadcast.29, bf16[9,128,128]{2,1,0:T(8,128)(2,1)S(1)} %bitcast.103, bf16[9,128,128]{2,1,0:T(8,128)(2,1)S(1)} %bitcast.102, bf16[9,128,128]{2,1,0:T(8,128)(2,1)S(1)} %bitcast.101, bf16[9,128,128]{2,1,0:T(8,128)(2,1)S(1)} %bitcast.100, ...), kind=kLoop, calls=%fused_computation.6 | loop fusion | flops 35389440 | bytes 6782976 | tf_op jit(solution)/shard_map/concatenate | solution.py:55
  58.9 6.9 %maximum_maximum_fusion = bf16[9,768,256]{2,1,0:T(8,128)(2,1)} fusion(bf16[9,384,64]{2,1,0:T(8,128)(2,1)S(1)} %get-tuple-element.56, bf16[9,384,64]{2,1,0:T(8,128)(2,1)S(1)} %copy-done.3, bf16[9,192,64]{2,1,0:T(8,128)(2,1)S(1)} %broadcast.26, bf16[9,64,64]{2,1,0:T(8,128)(2,1)S(1)} %bitcast.97, bf16[9,64,64]{2,1,0:T(8,128)(2,1)S(1)} %bitcast.96, ...), kind=kLoop, calls=%fused_computation | loop fusion | flops 70778880 | bytes 5971968 | tf_op jit(solution)/shard_map/concatenate | solution.py:67
  70.9 3.3 %collective-permute-start.4 = (bf16[20,8,48]{1,2,0:T(8,128)(2,1)S(1)}, bf16[20,8,48]{1,2,0:T(8,128)(2,1)S(1)}, u32[]{:S(2)}, u32[]{:S(2)}) collective-permute-start(bf16[20,8,48]{1,2,0:T(8,128)(2,1)S(1)} %get-tuple-element.30), channel_id=1, source_target_pairs={{0,8},{8,16},{16,24},{24,0},{1,9},{9,17},{17,25},{25,1},{2,10},{10... | collective-permute-start | bytes 46088 | tf_op jit(solution)/shard_map/ppermute | solution.py:14
  74.2 3.3 %collective-permute-start.5 = (bf16[20,8,48]{1,2,0:T(8,128)(2,1)S(1)}, bf16[20,8,48]{1,2,0:T(8,128)(2,1)S(1)}, u32[]{:S(2)}, u32[]{:S(2)}) collective-permute-start(bf16[20,8,48]{1,2,0:T(8,128)(2,1)S(1)} %get-tuple-element.31), channel_id=1, source_target_pairs={{0,24},{8,0},{16,8},{24,16},{1,25},{9,1},{17,9},{25,17},{2,26},{10... | collective-permute-start | bytes 46088 | tf_op jit(solution)/shard_map/ppermute | solution.py:14
  77.9 6.0 %collective-permute-done.4 = bf16[20,8,48]{1,2,0:T(8,128)(2,1)S(1)} collective-permute-done((bf16[20,8,48]{1,2,0:T(8,128)(2,1)S(1)}, bf16[20,8,48]{1,2,0:T(8,128)(2,1)S(1)}, u32[]{:S(2)}, u32[]{:S(2)}) %collective-permute-start.4) | collective-permute-done | bytes 15392 | tf_op jit(solution)/shard_map/ppermute | solution.py:14
  83.9 4.9 %collective-permute-done.5 = bf16[20,8,48]{1,2,0:T(8,128)(2,1)S(1)} collective-permute-done((bf16[20,8,48]{1,2,0:T(8,128)(2,1)S(1)}, bf16[20,8,48]{1,2,0:T(8,128)(2,1)S(1)}, u32[]{:S(2)}, u32[]{:S(2)}) %collective-permute-start.5) | collective-permute-done | bytes 15392 | tf_op jit(solution)/shard_map/ppermute | solution.py:14
  89.2 2.9 %collective-permute-start.7 = (bf16[20,48,24]{1,2,0:T(8,128)(2,1)S(1)}, bf16[20,48,24]{1,2,0:T(8,128)(2,1)S(1)}, u32[]{:S(2)}, u32[]{:S(2)}) collective-permute-start(bf16[20,48,24]{1,2,0:T(8,128)(2,1)S(1)} %pad_maximum_fusion.7), channel_id=1, source_target_pairs={{0,7},{1,0},{2,1},{3,2},{4,3},{5,4},{6,5},{7,6},{8,15},{9,8},{10,9... | collective-permute-start | bytes 138248 | tf_op jit(solution)/shard_map/ppermute | solution.py:14
  96.4 33.0 %shard_map.100 = f32[192,128]{1,0:T(8,128)} custom-call(f32[968,128]{1,0:T(8,128)} %fusion.15.d_ref, bf16[384,1024]{1,0:T(8,128)(2,1)} %constant.5.clone.s_ref, bf16[256,256]{1,0:T(8,128)(2,1)} %maximum_maximum_fusion.1.wl_ref, bf16[3456,256]{1,0:T(8,128)(2,1)} %bitcast.87, bf16[512,128]{1,0:T(8,128)(2,1)} %bitcast.115, bf16[4608,256]{1,0:T(8,128)(2,1)} %bitcast.84, ...), custom_call_target="tpu_custom_call" | custom-call | flops 20000000000 | bytes 20000000 | tf_op jit(solution)/shard_map/pallas_call | solution.py:227
  129.3 1.1 reshape.65
  (105 shorter events, 25.3 us)
Async XLA Ops:
  0.8 4.8 %copy-start.13 = (bf16[4,32,16]{1,2,0:T(8,128)(2,1)}, bf16[4,32,16]{1,2,0:T(8,128)(2,1)S(1)}, u32[]{:S(2)}) copy-start(bf16[4,32,16]{1,2,0:T(8,128)(2,1)S(1)} %get-tuple-element.51) | copy-start | bytes 12292
  0.8 4.8 %copy-start.14 = (bf16[4,32,16]{1,2,0:T(8,128)(2,1)}, bf16[4,32,16]{1,2,0:T(8,128)(2,1)S(1)}, u32[]{:S(2)}) copy-start(bf16[4,32,16]{1,2,0:T(8,128)(2,1)S(1)} %get-tuple-element.52) | copy-start | bytes 12292
  1.4 65.3 %collective-permute-start = (bf16[4,32,48]{1,2,0:T(8,128)(2,1)}, bf16[4,32,48]{1,2,0:T(8,128)(2,1)}, u32[]{:S(2)}, u32[]{:S(2)}) collective-permute-start(bf16[4,32,48]{1,2,0:T(8,128)(2,1)} %pad_maximum_fusion.8), channel_id=1, source_target_pairs={{0,64},{32,96},{64,128},{96,160},{128,192},{160,224},{192,0},{224,... | collective-permute-start | bytes 36872 | tf_op jit(solution)/shard_map/ppermute | solution.py:14
  3.5 64.0 %collective-permute-start.1 = (bf16[4,32,48]{1,2,0:T(8,128)(2,1)}, bf16[4,32,48]{1,2,0:T(8,128)(2,1)}, u32[]{:S(2)}, u32[]{:S(2)}) collective-permute-start(bf16[4,32,48]{1,2,0:T(8,128)(2,1)} %pad_maximum_fusion.8), channel_id=1, source_target_pairs={{0,32},{32,64},{64,96},{96,128},{128,160},{160,192},{192,224},{224... | collective-permute-start | bytes 36872 | tf_op jit(solution)/shard_map/ppermute | solution.py:14
  4.7 64.3 %collective-permute-start.2 = (bf16[4,32,48]{1,2,0:T(8,128)(2,1)}, bf16[4,32,48]{1,2,0:T(8,128)(2,1)}, u32[]{:S(2)}, u32[]{:S(2)}) collective-permute-start(bf16[4,32,48]{1,2,0:T(8,128)(2,1)} %pad_maximum_fusion.8), channel_id=1, source_target_pairs={{0,224},{32,0},{64,32},{96,64},{128,96},{160,128},{192,160},{224,1... | collective-permute-start | bytes 36872 | tf_op jit(solution)/shard_map/ppermute | solution.py:14
  5.6 64.4 %collective-permute-start.3 = (bf16[4,32,48]{1,2,0:T(8,128)(2,1)}, bf16[4,32,48]{1,2,0:T(8,128)(2,1)}, u32[]{:S(2)}, u32[]{:S(2)}) collective-permute-start(bf16[4,32,48]{1,2,0:T(8,128)(2,1)} %pad_maximum_fusion.8), channel_id=1, source_target_pairs={{0,192},{32,224},{64,0},{96,32},{128,64},{160,96},{192,128},{224,1... | collective-permute-start | bytes 36872 | tf_op jit(solution)/shard_map/ppermute | solution.py:14
  43.4 8.4 %copy-start.5 = (bf16[9,384,64]{2,1,0:T(8,128)(2,1)S(1)}, bf16[9,384,64]{2,1,0:T(8,128)(2,1)}, u32[]{:S(2)}) copy-start(bf16[9,384,64]{2,1,0:T(8,128)(2,1)} %broadcast_dynamic-update-slice_fusion.5) | copy-start | bytes 1327108
  47.3 8.8 %copy-start.6 = (bf16[9,1,128,128]{3,2,0,1:T(8,128)(2,1)S(1)}, bf16[9,1,128,128]{3,2,0,1:T(8,128)(2,1)}, u32[]{:S(2)}) copy-start(bf16[9,1,128,128]{3,2,0,1:T(8,128)(2,1)} %copy.83) | copy-start | bytes 884740
  47.3 8.8 %copy-start.7 = (bf16[9,1,128,128]{3,2,0,1:T(8,128)(2,1)S(1)}, bf16[9,1,128,128]{3,2,0,1:T(8,128)(2,1)}, u32[]{:S(2)}) copy-start(bf16[9,1,128,128]{3,2,0,1:T(8,128)(2,1)} %copy.84) | copy-start | bytes 884740
  47.3 8.8 %copy-start.8 = (bf16[9,1,128,128]{3,2,0,1:T(8,128)(2,1)S(1)}, bf16[9,1,128,128]{3,2,0,1:T(8,128)(2,1)}, u32[]{:S(2)}) copy-start(bf16[9,1,128,128]{3,2,0,1:T(8,128)(2,1)} %copy.85) | copy-start | bytes 884740
  47.3 8.8 %copy-start.9 = (bf16[9,1,128,128]{3,2,0,1:T(8,128)(2,1)S(1)}, bf16[9,1,128,128]{3,2,0,1:T(8,128)(2,1)}, u32[]{:S(2)}) copy-start(bf16[9,1,128,128]{3,2,0,1:T(8,128)(2,1)} %copy.86) | copy-start | bytes 884740
  47.3 8.8 %copy-start.10 = (bf16[9,1,128,128]{3,2,0,1:T(8,128)(2,1)S(1)}, bf16[9,1,128,128]{3,2,0,1:T(8,128)(2,1)}, u32[]{:S(2)}) copy-start(bf16[9,1,128,128]{3,2,0,1:T(8,128)(2,1)} %copy.87) | copy-start | bytes 884740
  47.3 8.8 %copy-start.11 = (bf16[9,1,128,128]{3,2,0,1:T(8,128)(2,1)S(1)}, bf16[9,1,128,128]{3,2,0,1:T(8,128)(2,1)}, u32[]{:S(2)}) copy-start(bf16[9,1,128,128]{3,2,0,1:T(8,128)(2,1)} %copy.88) | copy-start | bytes 884740
  56.0 2.8 %copy-start = (bf16[9,1,64,64]{3,2,0,1:T(8,128)(2,1)S(1)}, bf16[9,1,64,64]{3,2,0,1:T(8,128)(2,1)}, u32[]{:S(2)}) copy-start(bf16[9,1,64,64]{3,2,0,1:T(8,128)(2,1)} %copy.94) | copy-start | bytes 221188
  56.0 2.8 %copy-start.1 = (bf16[9,1,64,64]{3,2,0,1:T(8,128)(2,1)S(1)}, bf16[9,1,64,64]{3,2,0,1:T(8,128)(2,1)}, u32[]{:S(2)}) copy-start(bf16[9,1,64,64]{3,2,0,1:T(8,128)(2,1)} %copy.92) | copy-start | bytes 221188
  56.0 2.8 %copy-start.2 = (bf16[9,1,64,64]{3,2,0,1:T(8,128)(2,1)S(1)}, bf16[9,1,64,64]{3,2,0,1:T(8,128)(2,1)}, u32[]{:S(2)}) copy-start(bf16[9,1,64,64]{3,2,0,1:T(8,128)(2,1)} %copy.93) | copy-start | bytes 221188
  56.0 2.8 %copy-start.3 = (bf16[9,384,64]{2,1,0:T(8,128)(2,1)S(1)}, bf16[9,384,64]{2,1,0:T(8,128)(2,1)}, u32[]{:S(2)}) copy-start(bf16[9,384,64]{2,1,0:T(8,128)(2,1)} %get-tuple-element.53) | copy-start | bytes 1327108
  56.0 2.9 %copy-start.4 = (bf16[9,384,64]{2,1,0:T(8,128)(2,1)S(1)}, bf16[9,384,64]{2,1,0:T(8,128)(2,1)}, u32[]{:S(2)}) copy-start(bf16[9,384,64]{2,1,0:T(8,128)(2,1)} %get-tuple-element.54) | copy-start | bytes 1327108
  58.9 6.9 %copy-start.16 = (bf16[16,16]{0,1:T(8,128)(2,1)S(1)}, bf16[16,16]{0,1:T(8,128)(2,1)}, u32[]{:S(2)}) copy-start(bf16[16,16]{0,1:T(8,128)(2,1)} %fusion.25) | copy-start | bytes 1540
  58.9 6.9 %copy-start.17 = (bf16[3,64]{1,0:T(4,128)(2,1)S(1)}, bf16[3,64]{1,0:T(4,128)(2,1)}, u32[]{:S(2)}) copy-start(bf16[3,64]{1,0:T(4,128)(2,1)} %param.18) | copy-start | bytes 1156
  65.8 28.2 %copy-start.15 = (bf16[8,64,128]{2,1,0:T(8,128)(2,1)S(1)}, bf16[8,64,128]{2,1,0:T(8,128)(2,1)}, u32[]{:S(2)}) copy-start(bf16[8,64,128]{2,1,0:T(8,128)(2,1)} %param.16) | copy-start | bytes 393220
  70.9 13.1 %collective-permute-start.4 = (bf16[20,8,48]{1,2,0:T(8,128)(2,1)S(1)}, bf16[20,8,48]{1,2,0:T(8,128)(2,1)S(1)}, u32[]{:S(2)}, u32[]{:S(2)}) collective-permute-start(bf16[20,8,48]{1,2,0:T(8,128)(2,1)S(1)} %get-tuple-element.30), channel_id=1, source_target_pairs={{0,8},{8,16},{16,24},{24,0},{1,9},{9,17},{17,25},{25,1},{2,10},{10... | collective-permute-start | bytes 46088 | tf_op jit(solution)/shard_map/ppermute | solution.py:14
  74.2 14.6 %collective-permute-start.5 = (bf16[20,8,48]{1,2,0:T(8,128)(2,1)S(1)}, bf16[20,8,48]{1,2,0:T(8,128)(2,1)S(1)}, u32[]{:S(2)}, u32[]{:S(2)}) collective-permute-start(bf16[20,8,48]{1,2,0:T(8,128)(2,1)S(1)} %get-tuple-element.31), channel_id=1, source_target_pairs={{0,24},{8,0},{16,8},{24,16},{1,25},{9,1},{17,9},{25,17},{2,26},{10... | collective-permute-start | bytes 46088 | tf_op jit(solution)/shard_map/ppermute | solution.py:14
  89.1 5.8 %collective-permute-start.6 = (bf16[20,48,24]{1,2,0:T(8,128)(2,1)S(1)}, bf16[20,48,24]{1,2,0:T(8,128)(2,1)S(1)}, u32[]{:S(2)}, u32[]{:S(2)}) collective-permute-start(bf16[20,48,24]{1,2,0:T(8,128)(2,1)S(1)} %pad_maximum_fusion.6), channel_id=1, source_target_pairs={{0,1},{1,2},{2,3},{3,4},{4,5},{5,6},{6,7},{7,0},{8,9},{9,10},{10,1... | collective-permute-start | bytes 138248 | tf_op jit(solution)/shard_map/ppermute | solution.py:14
  89.2 5.9 %collective-permute-start.7 = (bf16[20,48,24]{1,2,0:T(8,128)(2,1)S(1)}, bf16[20,48,24]{1,2,0:T(8,128)(2,1)S(1)}, u32[]{:S(2)}, u32[]{:S(2)}) collective-permute-start(bf16[20,48,24]{1,2,0:T(8,128)(2,1)S(1)} %pad_maximum_fusion.7), channel_id=1, source_target_pairs={{0,7},{1,0},{2,1},{3,2},{4,3},{5,4},{6,5},{7,6},{8,15},{9,8},{10,9... | collective-permute-start | bytes 138248 | tf_op jit(solution)/shard_map/ppermute | solution.py:14
  96.3 34.4 %copy-start.12 = (bf16[3,4,32,16]{2,3,1,0:T(8,128)(2,1)S(1)}, bf16[3,4,32,16]{2,3,1,0:T(8,128)(2,1)}, u32[]{:S(2)}) copy-start(bf16[3,4,32,16]{2,3,1,0:T(8,128)(2,1)} %param.10) | copy-start | bytes 36868
where the time goes:
time: 134 us; the launch traced here: 131 us
  local copies, waits for them, and re-layouts  52.2 us (39%)
  Pallas kernels  33 us (25%)
  other arithmetic  18.7 us (14%)
  starting transfers between devices  16.2 us (12%)
  waiting for transfers between devices  10.9 us (8%)
    unnamed x70, local copies, waits for them, and re-layouts  34.9 us
    pallas_call x1, Pallas kernels, compute(): pl.pallas_call(kernel, out_shape=jax.ShapeDtypeStruct((192, 128), F32), i...  33 us
    ppermute x8, starting transfers between devices, shift(): lax.ppermute(block, axis, [(i, (i + step) % count) for i in range(count)])  16.2 us
    ppermute x8, waiting for transfers between devices, shift(): lax.ppermute(block, axis, [(i, (i + step) % count) for i in range(count)])  10.9 us
    concatenate x1, other arithmetic, weights(): wdec = jnp.concatenate([ws, wu], axis=1).reshape(6912, 256)  6.92 us
    slice x2, local copies, waits for them, and re-layouts, pair_matrix(): c0, c1, c2 = (t[:, 0], t[:, 1], t[:, 2])  4.16 us
    concatenate x1, other arithmetic, quad_matrix(): return jnp.concatenate([jnp.concatenate(c, axis=1) for c in cols], axis=2)  4.12 us
    slice x3, local copies, waits for them, and re-layouts, quad_matrix(): c0, c1, c2 = (t[:, 0], t[:, 1], t[:, 2])  3.39 us
  transfers between devices with their start and end apart: 8, of which 2 were waited for; matrix products, arithmetic and copies ran while one was open for 49% of the time, Pallas kernels for 0%

commit v1 on v0

v1 whole, which is shorter than its diff:
```python
import jax
import jax.numpy as jnp
import numpy as np
from jax import lax
from jax.experimental import pallas as pl
from jax.experimental.pallas import tpu as pltpu
from jax.sharding import PartitionSpec as P

BF, F32 = jnp.bfloat16, jnp.float32


def shift(block, axis, step):
    count = lax.axis_size(axis)
    return lax.ppermute(block, axis, [(i, (i + step) % count) for i in range(count)])


def act(value):
    return jnp.maximum(value, 0.1 * value)


def picker():
    table = np.zeros((3, 128, 8, 128), np.float32)
    for b in range(3):
        for q in range(8):
            for a in range(2):
                for ch in range(3):
                    for zi in range(6):
                        z = 4 * q + zi - 1
                        if 0 <= z < 32:
                            start = (48, 24 - 8, -16, 72 - 24)[z // 8]
                            table[b, start + 8 * ch + z, q, 18 * (3 * a + b) + 6 * ch + zi] = 1
    return table.reshape(384, 1024)


def lift_matrix(w):
    w = jnp.transpose(w.reshape(9, 3, 64, 3), (0, 3, 1, 2))
    cols = [jnp.pad(w, ((0, 0), (0, 0), (zo, 3 - zo), (0, 0))) for zo in range(4)]
    m = jnp.concatenate(cols, axis=3).reshape(162, 256)
    return jnp.concatenate([m[:108], jnp.zeros((20, 256), BF), m[108:], jnp.zeros((74, 256), BF)], axis=0)


def head_matrix(w):
    wt = w.T
    m = jnp.einsum("zs,ck->zcks", jnp.eye(16, dtype=BF), wt)
    return jnp.pad(m.reshape(1024, 48), ((0, 0), (0, 80)))


def banded_kernel(e_ref, d_ref, m1_ref, m2_ref, u_ref, j_ref, we, wd, w1, w2, wu, wj):
    def turned(value):
        return jnp.transpose(value.astype(F32)).astype(BF)

    def quad(raw, t, width):
        c = [raw[3 * t + k] for k in range(3)]
        o = jnp.zeros_like(c[0])
        blocks = [turned(jnp.concatenate(p, axis=0)) for p in ((c[0], o), (c[1], c[0]), (c[2], c[1]), (o, c[2]))]
        empty = jnp.zeros((width, 128), BF)
        order = (0, 1, 2, 3, 4, -1)
        return [[blocks[z - 2 * p + 1] if 0 <= z - 2 * p + 1 < 4 else empty for z in order] for p in range(2)]

    def step(t, carry):
        for p, column in enumerate(quad(e_ref, t, 64)):
            for k, block in enumerate(column):
                we[t, 64 * k:64 * k + 64, 128 * p:128 * p + 128] = block
        for p, column in enumerate(quad(j_ref, t, 128)):
            for k, block in enumerate(column):
                wj[t, 64 * k:64 * k + 64, 128 * p:128 * p + 128] = block[:64]
                wj[t, 384 + 64 * k:448 + 64 * k, 128 * p:128 * p + 128] = block[64:]
        for raw, out in ((m1_ref, w1), (m2_ref, w2)):
            c = [turned(raw[3 * t + k]) for k in range(3)]
            empty = jnp.zeros((128, 128), BF)
            for zo in range(2):
                for zi in range(4):
                    out[t, 128 * zi:128 * zi + 128, 128 * zo:128 * zo + 128] = c[zi - zo] if 0 <= zi - zo < 3 else empty
        return carry

    lax.fori_loop(0, 9, step, 0)
    for k in range(4):
        wd[128 * k:128 * k + 64] = turned(d_ref[2 * k])
        wd[128 * k + 64:128 * k + 128] = turned(d_ref[2 * k + 1])
        wu[:, 128 * k:128 * k + 128] = turned(jnp.concatenate([u_ref[2 * k], u_ref[2 * k + 1]], axis=0))


def weights(lift, encode, down, m1, m2, up, decode, head):
    shapes = ((9, 384, 256), (512, 128), (9, 512, 256), (9, 512, 256), (128, 512), (9, 768, 256))
    we, wd, w1, w2, wu, wj = pl.pallas_call(
        banded_kernel,
        out_shape=[jax.ShapeDtypeStruct(shape, BF) for shape in shapes],
        in_specs=[pl.BlockSpec(memory_space=pltpu.VMEM)] * 6,
        out_specs=[pl.BlockSpec(memory_space=pltpu.VMEM)] * 6,
        compiler_params=pltpu.CompilerParams(vmem_limit_bytes=40 << 20),
        cost_estimate=pl.CostEstimate(flops=5_000_000_000, bytes_accessed=14_000_000, transcendentals=0),
    )(encode, down, m1, m2, up, decode)
    return (
        lift_matrix(lift), we.reshape(3456, 256), wd, w1.reshape(4608, 256), w2.reshape(4608, 256),
        wu, wj.reshape(6912, 256), head_matrix(head),
    )


def dot(a, b):
    return jnp.dot(a, b, preferred_element_type=F32)


def rows(parts):
    flat = [p.reshape(-1, p.shape[-1]) for p in parts]
    return flat[0] if len(flat) == 1 else jnp.concatenate(flat, axis=1)


def up_one(v):
    return pltpu.roll(v, v.shape[-2] - 1, v.ndim - 2)


def plane_kernel(d_ref, a_ref, top_ref, low_ref):
    for x in range(4):
        parts = [d_ref[k, x].astype(F32)[h:h + 8] for h in (8, 0) for k in range(3)]
        t = jnp.transpose(jnp.concatenate(parts, axis=0))
        t = jnp.concatenate([t, jnp.zeros((32, 80), F32)], axis=1)
        a_ref[x] = t.astype(BF)
        top_ref[x] = t[24:].astype(BF)
        low_ref[x] = t[:8].astype(BF)


def join_kernel(before_ref, a_ref, after_ref, o_ref):
    for x in range(4):
        parts = [r[x].astype(F32) for r in (before_ref, a_ref, after_ref)]
        o_ref[x] = jnp.concatenate(parts, axis=0).astype(BF)


def rim_kernel(b0, b1, b2, b3, b4, left_ref, right_ref):
    lane = lax.broadcasted_iota(jnp.int32, (16, 128), 1)
    for x in range(20):
        own = (b0, b1, b2, b3, b4)[x // 4][x % 4].astype(F32)
        for out, first in ((left_ref, 0), (right_ref, 24)):
            g = [own[16 * k:16 * k + 16] for k in range(3)]
            g = [t if 24 * k == first else pltpu.roll(t, (24 * k - first) % 128, 1) for k, t in enumerate(g)]
            out[x] = jnp.where(lane < 24, g[0], jnp.where(lane < 48, g[1], g[2])).astype(BF)


def tiles(df, dt):
    for yo in range(8):
        for xo in range(12):
            t = [df[pl.ds((8 * xi + xo) * 48 + yo, 8, stride=6), :] for xi in range(2)]
            dt[yo, xo] = jnp.concatenate(t, axis=0).astype(BF)


def lift(dt, s_ref, wl_ref, db, fp, pairs, count, index):
    for one, two in pairs:
        if two == one + 1:
            table = s_ref[:, 128 * one:128 * one + 256]
        else:
            table = jnp.concatenate([s_ref[:, 128 * one:128 * one + 128], s_ref[:, 128 * two:128 * two + 128]], axis=1)
        r = dot(rows([dt[b:b + 6] for b in range(3)]), table)
        r = r.astype(BF).reshape(6, 12, 16, 256)
        db[one] = r[..., :128]
        db[two] = r[..., 128:]
    first_slots = lax.broadcasted_iota(jnp.int32, (16, 128), 1) < 54

    def step(i, carry):
        q = index(i)
        for g in range(2):
            y = slice(3 * g, 3 * g + 3)
            ta = jnp.where(first_slots, db[q, y, 0:10], db[q, y, 1:11])
            r = act(dot(rows([ta, db[q, y, 2:12]]), wl_ref[...]))
            for half in range(2):
                part = r[:, 128 * half:128 * half + 128].reshape(3, 10, 16, 128)
                fp[2 * q + half, y] = part.astype(BF)
                if g == 0:
                    low_rows = part[0:2].reshape(40, 8, 128)
                    fp[2 * q + half, 6:8] = up_one(low_rows).reshape(2, 10, 16, 128).astype(BF)
        return carry

    lax.fori_loop(0, count, step, 0)


def encode(fp, fe, we_ref, sk, sd, base, count, index):
    low = lax.broadcasted_iota(jnp.int32, (16, 128), 1) < 64

    def edge_step(i, carry):
        q = index(i)
        fe[q] = jnp.where(low, fp[2 * q + 3], fp[2 * q])
        return carry

    lax.fori_loop(0, count, edge_step, 0)

    def step(i, carry):
        q = index(i)
        for g in range(2):
            y0 = 3 * g
            acc = None
            for lo, hi in ((0, 2), (2, 4), (4, 6), (6, 9)):
                parts = []
                for t in range(lo, hi):
                    a, b = t // 3, t % 3
                    sl = (slice(y0 + b, y0 + b + 3), slice(a, a + 8))
                    parts += [fp[(2 * q + 1,) + sl], fp[(2 * q + 2,) + sl], fe[(q,) + sl]]
                p = dot(rows(parts), we_ref[384 * lo:384 * hi, :])
                acc = p if acc is None else acc + p
            r = act(acc).reshape(3, 8, 2, 8, 256)
            for half in range(2):
                part = r[..., 128 * half:128 * half + 128]
                packed = part.reshape(3, 8, 16, 128).astype(BF)
                sp = 2 * q + half - base
                for yy in range(3):
                    yo = y0 + yy
                    sk[sp, yo // 2, yo % 2] = packed[yy].reshape(4, 2, 16, 128)
                    mixed = [jnp.concatenate([part[yy, (5 + xo) % 8, (5 + xo) // 8], part[yy, (7 + xo) % 8, (7 + xo) // 8]], axis=0)
                             for xo in range(4)]
                    mixed = jnp.stack(mixed).reshape(8, 8, 128)
                    if yo == 5:
                        sd[sp, 0] = mixed.reshape(4, 16, 128).astype(BF)
                    moved = up_one(mixed)
                    sd[sp, yo + 1] = moved.reshape(4, 16, 128).astype(BF)
                    if yo == 0:
                        sd[sp, 7] = up_one(moved).reshape(4, 16, 128).astype(BF)
        return carry

    lax.fori_loop(0, count, step, 0)


def inner_kernel(b0, b1, b2, b3, b4, s_ref, wl_ref, we_hbm, sk, sd, df, dt, db, fp, fe, we_ref, sem):
    copy = pltpu.make_async_copy(we_hbm, we_ref, sem)
    copy.start()
    for k, ref in enumerate((b0, b1, b2, b3, b4)):
        for x in range(4):
            df[192 * k + 48 * x:192 * k + 48 * x + 48] = ref[x].astype(F32)
    df[960:968] = jnp.zeros((8, 128), F32)
    tiles(df, dt)
    lift(dt, s_ref, wl_ref, db, fp, ((2, 3), (4, 5)), 4, lambda i: i + 2)
    copy.wait()
    encode(fp, fe, we_ref, sk, sd, 4, 3, lambda i: i + 2)


def outer_kernel(b0, b1, b2, b3, b4, left_ref, right_ref, x_ref, s_ref, wl_ref,
                 we_hbm, wd_hbm, w1_hbm, w2_hbm, wu_hbm, wj_hbm, wh_hbm, sk_hbm, sd_hbm, o_ref,
                 df, dt, db, fp, fe, sk, sd, c1, c2, de, uu, es, eu, hs,
                 we_ref, wd_ref, w1_ref, w2_ref, wu_ref, wj_ref, wh_ref, sems):
    plan = ((we_hbm, we_ref), (sk_hbm, sk.at[4:10]), (wd_hbm, wd_ref), (w1_hbm, w1_ref), (w2_hbm, w2_ref),
            (wu_hbm, wu_ref), (sd_hbm, sd.at[4:10]), (wj_hbm, wj_ref), (wh_hbm, wh_ref))
    copies = [pltpu.make_async_copy(src, dst, sems.at[i]) for i, (src, dst) in enumerate(plan)]
    for copy in copies:
        copy.start()

    lane = lax.broadcasted_iota(jnp.int32, (16, 128), 1)
    low = lane < 64
    for x in range(20):
        own = (b0, b1, b2, b3, b4)[x // 4][x % 4].astype(F32)
        left, right = left_ref[x].astype(F32), right_ref[x].astype(F32)
        for g in range(3):
            t = jnp.where(lane < 72, pltpu.roll(left, 48 - 24 * g if g < 2 else 0, 1) if g < 2 else left,
                          pltpu.roll(right, 72 - 24 * g, 1))
            df[48 * x + 16 * g:48 * x + 16 * g + 16] = jnp.where(lane < 48, own[16 * g:16 * g + 16], t)
    df[960:968] = jnp.zeros((8, 128), F32)
    tiles(df, dt)
    lift(dt, s_ref, wl_ref, db, fp, ((0, 1), (2, 5), (6, 7)), 6, lambda i: i + 2 * (i // 3))
    copies[0].wait()
    encode(fp, fe, we_ref, sk, sd, 0, 4, lambda i: i + 3 * (i // 2))

    copies[1].wait()
    copies[2].wait()
    r = act(dot(rows([sk[:, :, b, :, a] for a in range(2) for b in range(2)]), wd_ref[...]))
    r = r.reshape(7, 2, 3, 4, 2, 8, 128)
    for yo in range(3):
        for xo in range(5):
            t = jnp.stack([r[:, :, yo, xo % 4, xo // 4], r[:, :, yo, (3 + xo) % 4, (3 + xo) // 4]], axis=2)
            c1[:, :, yo, xo] = t.reshape(7, 2, 16, 128).astype(BF)
            if yo < 2:
                c1[:, :, yo + 3, xo] = up_one(t.reshape(28, 8, 128)).reshape(7, 2, 16, 128).astype(BF)

    def middle(src, w_ref, zp, xn):
        acc = None
        for t in range(9):
            a, b = t // 3, t % 3
            parts = [src[zi // 2:zi // 2 + zp, zi % 2, b:b + 3, a:a + xn] for zi in range(4)]
            p = dot(rows(parts), w_ref[512 * t:512 * t + 512, :])
            acc = p if acc is None else acc + p
        return act(acc).reshape(zp, 3, xn, 2, 8, 256)

    copies[3].wait()
    r = middle(c1, w1_ref, 6, 3)
    for half in range(2):
        part = r[..., 128 * half:128 * half + 128]
        for yo in range(3):
            for xo in range(4):
                t = jnp.stack([part[:, yo, xo % 3, xo // 3], part[:, yo, (2 + xo) % 3, (2 + xo) // 3]], axis=1)
                c2[:, half, yo, xo] = t.reshape(6, 16, 128).astype(BF)
                if yo < 2:
                    c2[:, half, yo + 3, xo] = up_one(t.reshape(12, 8, 128)).reshape(6, 16, 128).astype(BF)

    copies[4].wait()
    r = middle(c2, w2_ref, 5, 2).reshape(5, 3, 2, 16, 256).astype(BF)
    de[:, 0] = r[..., :128]
    de[:, 1] = r[..., 128:]

    copies[5].wait()
    r = act(dot(rows([de[...]]), wu_ref[...])).reshape(5, 2, 3, 2, 2, 8, 512)
    for yo in range(6):
        b = yo % 2
        for xo in range(4):
            t = []
            for f in (1 + xo, 3 + xo):
                a = f % 2
                n = 128 * (2 * a + b)
                t.append(r[:, :, yo // 2, (f // 2) % 2, f // 4, :, n:n + 128])
            t = jnp.stack(t, axis=2)
            if yo > 0:
                uu[:, :, yo - 1, xo] = t.reshape(5, 2, 16, 128).astype(BF)
            if yo < 3:
                uu[:, :, yo + 5, xo] = up_one(t.reshape(20, 8, 128)).reshape(5, 2, 16, 128).astype(BF)

    for k in (6, 7, 8):
        copies[k].wait()
    for q in range(4):
        es[q] = jnp.where(low, sd[2 * q + 5], sd[2 * q + 2])
        eu[q] = jnp.where(low, uu[q + 1, 1], uu[q, 0])

    for g in range(1):
        acc = None
        for t in range(9):
            a, b = t // 3, t % 3
            ys, xs = slice(b, b + 6), slice(a, a + 2)
            own = [jnp.stack([sd[2 * q + 3 + k, ys, xs] for q in range(4)]) for k in range(2)]
            parts = own + [es[:, ys, xs], uu[0:4, 1, ys, xs], uu[1:5, 0, ys, xs], eu[:, ys, xs]]
            p = dot(rows(parts), wj_ref[768 * t:768 * t + 768, :])
            acc = p if acc is None else acc + p
        j = act(acc).astype(BF).reshape(4, 192, 256)
        h = dot(jnp.concatenate([j[q] for q in range(4)], axis=1), wh_ref[...]).reshape(6, 2, 2, 8, 128)
        for yo in range(6):
            for x in range(4):
                hs[pl.ds(48 * x + yo, 8, stride=6), :] = h[yo, x % 2, x // 2]
    for x in range(4):
        t = jnp.transpose(hs[48 * x:48 * x + 32, :])
        for k in range(3):
            o_ref[k, x] = t[16 * k:16 * k + 16] + x_ref[k, x].astype(F32)


VM = pl.BlockSpec(memory_space=pltpu.VMEM)
ANY = pl.BlockSpec(memory_space=pl.ANY)


def call(body, args, specs, shapes, scratch=(), limit=16, flops=1_000_000):
    many = isinstance(shapes, list)
    return pl.pallas_call(
        body,
        out_shape=[jax.ShapeDtypeStruct(*x) for x in shapes] if many else jax.ShapeDtypeStruct(*shapes),
        in_specs=specs,
        out_specs=[VM] * len(shapes) if many else VM,
        scratch_shapes=scratch,
        compiler_params=pltpu.CompilerParams(vmem_limit_bytes=limit << 20),
        cost_estimate=pl.CostEstimate(flops=flops, bytes_accessed=2_000_000, transcendentals=0),
    )(*args)


def planes(d):
    return call(plane_kernel, (d,), [VM], [((4, 32, 128), BF), ((4, 8, 128), BF), ((4, 8, 128), BF)])


def rims(blocks):
    return call(rim_kernel, blocks, [VM] * 5, [((20, 16, 128), BF)] * 2)


V = pltpu.VMEM
FIELDS = [V((968, 128), F32), V((8, 12, 16, 128), BF), V((8, 6, 12, 16, 128), BF), V((16, 8, 10, 16, 128), BF), V((7, 8, 10, 16, 128), BF)]
PICK = picker()


def inner(blocks, ws):
    args = (*blocks, jnp.asarray(PICK, BF), ws[0], ws[1])
    return call(
        inner_kernel, args, [VM] * 7 + [ANY], [((6, 3, 2, 4, 2, 16, 128), BF), ((6, 8, 4, 16, 128), BF)],
        FIELDS + [V((3456, 256), BF), pltpu.SemaphoreType.DMA], limit=24, flops=8_000_000_000,
    )


def outer(blocks, left, right, d, ws, sk, sd):
    args = (*blocks, left, right, d, jnp.asarray(PICK, BF), *ws, sk, sd)
    return call(
        outer_kernel, args, [VM] * 10 + [ANY] * 9, ((3, 4, 16, 32), F32),
        FIELDS + [
            V((14, 3, 2, 4, 2, 16, 128), BF), V((14, 8, 4, 16, 128), BF), V((7, 2, 5, 5, 16, 128), BF),
            V((6, 2, 5, 4, 16, 128), BF), V((5, 2, 3, 2, 16, 128), BF), V((5, 2, 8, 4, 16, 128), BF),
            V((4, 8, 4, 16, 128), BF), V((4, 8, 4, 16, 128), BF), V((192, 128), F32),
            V((3456, 256), BF), V((512, 128), BF), V((4608, 256), BF), V((4608, 256), BF), V((128, 512), BF), V((6912, 256), BF),
            V((1024, 128), BF), pltpu.SemaphoreType.DMA((9,)),
        ], limit=44, flops=16_000_000_000,
    )


def local(displacement, *raw):
    d = jnp.swapaxes(displacement, 2, 3)
    own, top, bottom = planes(d)
    before, after = shift(top, "gy", 1), shift(bottom, "gy", -1)
    ws = weights(*raw)
    block = call(join_kernel, (before, own, after), [VM] * 3, ((4, 48, 128), BF))
    blocks = (shift(block, "gx", 2), shift(block, "gx", 1), block, shift(block, "gx", -1), shift(block, "gx", -2))
    left, right = rims(blocks)
    left, right = shift(left, "gz", 1), shift(right, "gz", -1)
    sk, sd = inner(blocks, ws)
    return jnp.swapaxes(outer(blocks, left, right, d, ws, sk, sd), 2, 3)


def solution(mesh):
    placed = (P(None, "gx", "gy", "gz"), P(), P(), P(), P(), P(), P(), P(), P())
    return jax.shard_map(local, mesh=mesh, in_specs=placed, out_specs=P(None, "gx", "gy", "gz"), check_vma=False)
```

time: 134 us -> 76.6 us (0.57); the launches traced: 131 us -> 76.1 us
  local copies, waits for them, and re-layouts: 52.2 us -> 21 us
  other arithmetic: 18.7 us -> 2.54 us
  waiting for transfers between devices: 10.9 us -> 0.02 us
  Pallas kernels: 33 us -> 35 us
    unnamed x70 -> x37, local copies, waits for them, and re-layouts: 34.9 us -> 14.3 us
    concatenate x7 -> x0, other arithmetic: 14.7 us -> none  [the longest x1 6.92 us: weights(): wdec = jnp.concatenate([ws, wu], axis=1).reshape(6912, 256)]
    ppermute x8, waiting for transfers between devices: 10.9 us -> 0.02 us  [shift(): lax.ppermute(block, axis, [(i, (i + step) % count) for i in range(count)])]
    slice x9 -> x0, local copies, waits for them, and re-layouts: 9.1 us -> none  [the longest x2 4.16 us: pair_matrix(): c0, c1, c2 = (t[:, 0], t[:, 1], t[:, 2])]
    reshape x2, local copies, waits for them, and re-layouts: 0.34 us -> 3.49 us  [head_matrix(): return jnp.pad(m.reshape(1024, 48), ((0, 0), (0, 80)))]
    concatenate x6 -> x0, local copies, waits for them, and re-layouts: 2.82 us -> none  [the longest x4 1.85 us: quad_matrix(): return jnp.concatenate([jnp.concatenate(c, axis=1) for c in cols], axis=2)]
    pallas_call x1 -> x6, Pallas kernels: 33 us -> 35 us  [the longest x5 32.7 us: call(): pl.pallas_call(body, out_shape=[jax.ShapeDtypeStruct(*x) for x in shapes]...]
    reshape x2 -> x0, local copies, waits for them, and re-layouts: 1.84 us -> none  [the longest x1 1.08 us: compute(): out = out[:, :48].reshape(6, 2, 2, 8, 3, 16)]
  transfers between devices with their start and end apart: 8 -> 8, of which waited for: 2 -> 0; matrix products, arithmetic and copies ran while one was open for 49% -> 14% of each run, Pallas kernels for 0% -> 13%
where the time goes in v1:
time: 76.6 us; the launch traced here: 76.1 us
  Pallas kernels  35 us (46%)
  local copies, waits for them, and re-layouts  21 us (27%)
  starting transfers between devices  17.2 us (22%)
  other arithmetic  2.54 us (3%)
    pallas_call x5, Pallas kernels, call(): pl.pallas_call(body, out_shape=[jax.ShapeDtypeStruct(*x) for x in shapes]...  32.7 us
    ppermute x8, starting transfers between devices, shift(): lax.ppermute(block, axis, [(i, (i + step) % count) for i in range(count)])  17.2 us
    unnamed x37, local copies, waits for them, and re-layouts  14.3 us
    reshape x2, local copies, waits for them, and re-layouts, head_matrix(): return jnp.pad(m.reshape(1024, 48), ((0, 0), (0, 80)))  3.49 us
    pallas_call x1, Pallas kernels, weights(): pl.pallas_call(banded_kernel, out_shape=[jax.ShapeDtypeStruct(shape, BF)...  2.25 us
  transfers between devices with their start and end apart: 8, of which 0 were waited for; matrix products, arithmetic and copies ran while one was open for 14% of the time, Pallas kernels for 13%

profile of v1, /device:TPU:2, one launch (start us, length us, event | category | flops | bytes accessed | tf_op | source)
XLA Modules:
  0.0 76.1 jit_solution(9523487728334830252)
XLA Ops:
  0.0 0.8 %copy-done = bf16[3,4,32,16]{2,3,1,0:T(8,128)(2,1)S(1)} copy-done((bf16[3,4,32,16]{2,3,1,0:T(8,128)(2,1)S(1)}, bf16[3,4,32,16]{2,3,1,0:T(8,128)(2,1)}, u32[]{:S(2)}) %copy-start) | copy-done | bytes 12312
  0.9 3.3 %collective-permute-start = (bf16[4,8,128]{2,1,0:T(8,128)(2,1)S(1)}, bf16[4,8,128]{2,1,0:T(8,128)(2,1)S(1)}, u32[]{:S(2)}, u32[]{:S(2)}) collective-permute-start(bf16[4,8,128]{2,1,0:T(8,128)(2,1)S(1)} %get-tuple-element.18), channel_id=1, source_target_pairs={{0,8},{8,16},{16,24},{24,0},{1,9},{9,17},{17,25},{25,1},{2,10},{10... | collective-permute-start | bytes 24584 | tf_op jit(solution)/shard_map/ppermute | solution.py:14
  4.2 3.1 %collective-permute-start.1 = (bf16[4,8,128]{2,1,0:T(8,128)(2,1)S(1)}, bf16[4,8,128]{2,1,0:T(8,128)(2,1)S(1)}, u32[]{:S(2)}, u32[]{:S(2)}) collective-permute-start(bf16[4,8,128]{2,1,0:T(8,128)(2,1)S(1)} %get-tuple-element.20), channel_id=1, source_target_pairs={{0,24},{8,0},{16,8},{24,16},{1,25},{9,1},{17,9},{25,17},{2,26},{10... | collective-permute-start | bytes 24584 | tf_op jit(solution)/shard_map/ppermute | solution.py:14
  7.4 0.8 reshape.21
  8.1 1.1 %copy.16.d_ref = bf16[8,128,64]{2,1,0:T(8,128)(2,1)S(1)} copy(bf16[8,128,64]{1,2,0:T(8,128)(2,1)} %param.14) | data formatting | bytes 262144 | tf_op args[3]
  9.2 1.5 %multiply_bitcast_fusion = bf16[16,64,3,16]{1,0,3,2:T(8,128)(2,1)} fusion(bf16[64,3]{0,1:T(4,128)(2,1)} %bitcast.26, bf16[16,16]{0,1:T(8,128)(2,1)S(1)} %fusion.9), kind=kLoop, calls=%fused_computation.12 | loop fusion | flops 49152 | bytes 99200 | tf_op jit(solution)/shard_map/zs,ck->zcks/transpose | solution.py:44
  10.7 1.2 %copy-done.2 = bf16[27,128,128]{2,1,0:T(8,128)(2,1)S(1)} copy-done((bf16[27,128,128]{2,1,0:T(8,128)(2,1)S(1)}, bf16[27,128,128]{2,1,0:T(8,128)(2,1)}, u32[]{:S(2)}) %copy-start.2) | copy-done | bytes 884760
  11.9 1.2 %copy-done.3 = bf16[27,128,128]{2,1,0:T(8,128)(2,1)S(1)} copy-done((bf16[27,128,128]{2,1,0:T(8,128)(2,1)S(1)}, bf16[27,128,128]{2,1,0:T(8,128)(2,1)}, u32[]{:S(2)}) %copy-start.3) | copy-done | bytes 884760
  13.0 1.0 %copy-done.4 = bf16[27,64,64]{2,1,0:T(8,128)(2,1)S(1)} copy-done((bf16[27,64,64]{2,1,0:T(8,128)(2,1)S(1)}, bf16[27,64,64]{2,1,0:T(8,128)(2,1)}, u32[]{:S(2)}) %copy-start.4) | copy-done | bytes 221208
  14.0 1.0 %copy-done.5 = bf16[27,64,128]{2,1,0:T(8,128)(2,1)S(1)} copy-done((bf16[27,64,128]{2,1,0:T(8,128)(2,1)S(1)}, bf16[27,64,128]{2,1,0:T(8,128)(2,1)}, u32[]{:S(2)}) %copy-start.5) | copy-done | bytes 442392
  15.1 0.9 %copy-done.6 = bf16[8,64,128]{2,1,0:T(8,128)(2,1)S(1)} copy-done((bf16[8,64,128]{2,1,0:T(8,128)(2,1)S(1)}, bf16[8,64,128]{2,1,0:T(8,128)(2,1)}, u32[]{:S(2)}) %copy-start.6) | copy-done | bytes 131096
  16.0 2.3 %shard_map.112 = (bf16[9,384,256]{2,1,0:T(8,128)(2,1)S(1)}, bf16[512,128]{1,0:T(8,128)(2,1)S(1)}, bf16[9,512,256]{2,1,0:T(8,128)(2,1)S(1)}, bf16[9,512,256]{2,1,...) custom-call(bf16[27,64,64]{2,1,0:T(8,128)(2,1)S(1)} %copy-done.4, ...), custom_call_target="tpu_custom_call" | custom-call | flops 5000000000 | bytes 14000000 | tf_op jit(solution)/shard_map/pallas_call | solution.py:85
  18.2 1.7 %copy-done.7 = bf16[9,768,256]{2,1,0:T(8,128)(2,1)} copy-done((bf16[9,768,256]{2,1,0:T(8,128)(2,1)}, bf16[9,768,256]{2,1,0:T(8,128)(2,1)S(1)}, u32[]{:S(2)}) %copy-start.7) | copy-done | bytes 3538968
  20.0 1.4 %copy-done.8 = bf16[9,512,256]{2,1,0:T(8,128)(2,1)} copy-done((bf16[9,512,256]{2,1,0:T(8,128)(2,1)}, bf16[9,512,256]{2,1,0:T(8,128)(2,1)S(1)}, u32[]{:S(2)}) %copy-start.8) | copy-done | bytes 2359320
  21.4 1.2 %copy-done.10 = bf16[9,384,256]{2,1,0:T(8,128)(2,1)} copy-done((bf16[9,384,256]{2,1,0:T(8,128)(2,1)}, bf16[9,384,256]{2,1,0:T(8,128)(2,1)S(1)}, u32[]{:S(2)}) %copy-start.10) | copy-done | bytes 1769496
  22.6 0.6 copy-done.14
  23.2 0.7 copy-done.16
  24.1 0.7 pad.26.clone
  24.8 0.6 slice.13
  25.5 2.7 %collective-permute-start.5 = (bf16[4,48,128]{2,1,0:T(8,128)(2,1)S(1)}, bf16[4,48,128]{2,1,0:T(8,128)(2,1)S(1)}, u32[]{:S(2)}, u32[]{:S(2)}) collective-permute-start(bf16[4,48,128]{2,1,0:T(8,128)(2,1)S(1)} %shard_map.110.b2), channel_id=1, source_target_pairs={{0,192},{32,224},{64,0},{96,32},{128,64},{160,96},{192,128},{224,1... | collective-permute-start | bytes 147464 | tf_op jit(solution)/shard_map/ppermute | solution.py:14
  28.1 1.4 %collective-permute-start.4 = (bf16[4,48,128]{2,1,0:T(8,128)(2,1)S(1)}, bf16[4,48,128]{2,1,0:T(8,128)(2,1)S(1)}, u32[]{:S(2)}, u32[]{:S(2)}) collective-permute-start(bf16[4,48,128]{2,1,0:T(8,128)(2,1)S(1)} %shard_map.110.b2), channel_id=1, source_target_pairs={{0,224},{32,0},{64,32},{96,64},{128,96},{160,128},{192,160},{224,1... | collective-permute-start | bytes 147464 | tf_op jit(solution)/shard_map/ppermute | solution.py:14
  29.6 0.6 collective-permute-start.3
  30.2 3.1 %collective-permute-start.2 = (bf16[4,48,128]{2,1,0:T(8,128)(2,1)S(1)}, bf16[4,48,128]{2,1,0:T(8,128)(2,1)S(1)}, u32[]{:S(2)}, u32[]{:S(2)}) collective-permute-start(bf16[4,48,128]{2,1,0:T(8,128)(2,1)S(1)} %shard_map.110.b2), channel_id=1, source_target_pairs={{0,64},{32,96},{64,128},{96,160},{128,192},{160,224},{192,0},{224,... | collective-permute-start | bytes 147464 | tf_op jit(solution)/shard_map/ppermute | solution.py:14
  33.2 1.0 %maximum_maximum_fusion.wl_ref = bf16[256,256]{1,0:T(8,128)(2,1)S(1)} fusion(bf16[54,256]{1,0:T(8,128)(2,1)S(1)} %slice.15, bf16[108,256]{1,0:T(8,128)(2,1)} %slice.13, bf16[256]{0:T(256)(128)(2,1)S(1)} %pad.28.clone, bf16[256]{0:T(256)(128)(2,1)} %pad.26.clone), kind=kLoop, calls=%fused_computation.13 | loop fusion | flops 524288 | bytes 215040 | tf_op jit(solution)/shard_map/concatenate | solution.py:39
  34.2 1.7 %reshape.26 = bf16[1024,48]{0,1:T(8,128)(2,1)} reshape(bf16[16,64,3,16]{1,0,3,2:T(8,128)(2,1)} %multiply_bitcast_fusion) | data formatting | bytes 196608 | tf_op jit(solution)/shard_map/reshape | solution.py:45
  35.9 1.7 %copy.17 = bf16[1024,48]{1,0:T(8,128)(2,1)} copy(bf16[1024,48]{0,1:T(8,128)(2,1)} %reshape.26) | data formatting | bytes 196608 | tf_op jit(solution)/shard_map/reshape | solution.py:45
  37.7 1.0 %pad.24.wh_hbm = bf16[1024,128]{1,0:T(8,128)(2,1)S(1)} pad(bf16[1024,48]{1,0:T(8,128)(2,1)} %copy.17, bf16[]{:T(256)} %constant.2.clone.1), padding=0_0x0_80 | pad | bytes 360450 | tf_op jit(solution)/shard_map/jit(_pad)/pad | solution.py:45
  38.7 0.2 shard_map.111
  38.9 2.9 %collective-permute-start.7 = (bf16[20,16,128]{2,1,0:T(8,128)(2,1)S(1)}, bf16[20,16,128]{2,1,0:T(8,128)(2,1)S(1)}, u32[]{:S(2)}, u32[]{:S(2)}) collective-permute-start(bf16[20,16,128]{2,1,0:T(8,128)(2,1)S(1)} %get-tuple-element.22), channel_id=1, source_target_pairs={{0,7},{1,0},{2,1},{3,2},{4,3},{5,4},{6,5},{7,6},{8,15},{9,8},{10,9... | collective-permute-start | bytes 245768 | tf_op jit(solution)/shard_map/ppermute | solution.py:14
  41.9 1.5 %copy-done.11 = bf16[9,384,256]{2,1,0:T(8,128)(2,1)S(1)} copy-done((bf16[9,384,256]{2,1,0:T(8,128)(2,1)S(1)}, bf16[9,384,256]{2,1,0:T(8,128)(2,1)}, u32[]{:S(2)}) %copy-start.11) | copy-done | bytes 1769496
  43.4 7.4 %shard_map.113 = (bf16[6,3,2,4,2,16,128]{6,5,4,3,2,1,0:T(8,128)(2,1)S(1)}, bf16[6,8,4,16,128]{4,3,2,1,0:T(8,128)(2,1)S(1)}) custom-call(bf16[4,48,128]{2,1,0:T(8,128)(2,1)S(1)} %collective-permute-done.2.b0, bf16[4,48,128]{2,1,0:T(8,128)(2,1)S(1)} %collective-permute-done.3.b1, bf16[4,48,128]{2,1,0:T(8,128)(2,1)S(1)} %shard_map.110.b2, ...), custom_call_target="tpu_custom_call" | custom-call | flops 8000000000 | bytes 2000000 | tf_op jit(solution)/shard_map/pallas_call | solution.py:341
  50.9 25.1 %shard_map.114 = f32[3,4,16,32]{3,2,1,0:T(8,128)} custom-call(bf16[4,48,128]{2,1,0:T(8,128)(2,1)S(1)} %collective-permute-done.2.b0, bf16[4,48,128]{2,1,0:T(8,128)(2,1)S(1)} %collective-permute-done.3.b1, bf16[4,48,128]{2,1,0:T(8,128)(2,1)S(1)} %shard_map.110.b2, bf16[4,48,128]{2,1,0:T(8,128)(2,1)S(1)} %collective-permute-done.4.b3, ...), custom_call_target="tpu_custom_call" | custom-call | flops 16000000000 | bytes 2000000 | tf_op jit(solution)/shard_map/pallas_call | solution.py:341
  (44 shorter events, 0.4 us)
Async XLA Ops:
  0.0 0.8 %copy-start = (bf16[3,4,32,16]{2,3,1,0:T(8,128)(2,1)S(1)}, bf16[3,4,32,16]{2,3,1,0:T(8,128)(2,1)}, u32[]{:S(2)}) copy-start(bf16[3,4,32,16]{2,3,1,0:T(8,128)(2,1)} %param.11) | copy-start | bytes 36868
  0.9 24.6 %collective-permute-start = (bf16[4,8,128]{2,1,0:T(8,128)(2,1)S(1)}, bf16[4,8,128]{2,1,0:T(8,128)(2,1)S(1)}, u32[]{:S(2)}, u32[]{:S(2)}) collective-permute-start(bf16[4,8,128]{2,1,0:T(8,128)(2,1)S(1)} %get-tuple-element.18), channel_id=1, source_target_pairs={{0,8},{8,16},{16,24},{24,0},{1,9},{9,17},{17,25},{25,1},{2,10},{10... | collective-permute-start | bytes 24584 | tf_op jit(solution)/shard_map/ppermute | solution.py:14
  4.2 21.2 %collective-permute-start.1 = (bf16[4,8,128]{2,1,0:T(8,128)(2,1)S(1)}, bf16[4,8,128]{2,1,0:T(8,128)(2,1)S(1)}, u32[]{:S(2)}, u32[]{:S(2)}) collective-permute-start(bf16[4,8,128]{2,1,0:T(8,128)(2,1)S(1)} %get-tuple-element.20), channel_id=1, source_target_pairs={{0,24},{8,0},{16,8},{24,16},{1,25},{9,1},{17,9},{25,17},{2,26},{10... | collective-permute-start | bytes 24584 | tf_op jit(solution)/shard_map/ppermute | solution.py:14
  10.7 1.2 %copy-start.2 = (bf16[27,128,128]{2,1,0:T(8,128)(2,1)S(1)}, bf16[27,128,128]{2,1,0:T(8,128)(2,1)}, u32[]{:S(2)}) copy-start(bf16[27,128,128]{2,1,0:T(8,128)(2,1)} %m1_ref.1) | copy-start | bytes 2654212
  11.9 1.2 %copy-start.3 = (bf16[27,128,128]{2,1,0:T(8,128)(2,1)S(1)}, bf16[27,128,128]{2,1,0:T(8,128)(2,1)}, u32[]{:S(2)}) copy-start(bf16[27,128,128]{2,1,0:T(8,128)(2,1)} %m2_ref.1) | copy-start | bytes 2654212
  13.0 1.0 %copy-start.4 = (bf16[27,64,64]{2,1,0:T(8,128)(2,1)S(1)}, bf16[27,64,64]{2,1,0:T(8,128)(2,1)}, u32[]{:S(2)}) copy-start(bf16[27,64,64]{2,1,0:T(8,128)(2,1)} %e_ref.1) | copy-start | bytes 663556
  14.0 1.0 %copy-start.5 = (bf16[27,64,128]{2,1,0:T(8,128)(2,1)S(1)}, bf16[27,64,128]{2,1,0:T(8,128)(2,1)}, u32[]{:S(2)}) copy-start(bf16[27,64,128]{2,1,0:T(8,128)(2,1)} %j_ref.1) | copy-start | bytes 1327108
  15.1 0.9 %copy-start.6 = (bf16[8,64,128]{2,1,0:T(8,128)(2,1)S(1)}, bf16[8,64,128]{2,1,0:T(8,128)(2,1)}, u32[]{:S(2)}) copy-start(bf16[8,64,128]{2,1,0:T(8,128)(2,1)} %u_ref.1) | copy-start | bytes 393220
  16.0 25.9 %copy-start.13 = (bf16[384,1024]{1,0:T(8,128)(2,1)S(1)}, bf16[384,1024]{1,0:T(8,128)(2,1)}, u32[]{:S(2)}) copy-start(bf16[384,1024]{1,0:T(8,128)(2,1)} %constant.3.clone.s_ref) | copy-start | bytes 2359300
  18.2 1.7 %copy-start.7 = (bf16[9,768,256]{2,1,0:T(8,128)(2,1)}, bf16[9,768,256]{2,1,0:T(8,128)(2,1)S(1)}, u32[]{:S(2)}) copy-start(bf16[9,768,256]{2,1,0:T(8,128)(2,1)S(1)} %get-tuple-element.28) | copy-start | bytes 10616836
  20.0 1.4 %copy-start.8 = (bf16[9,512,256]{2,1,0:T(8,128)(2,1)}, bf16[9,512,256]{2,1,0:T(8,128)(2,1)S(1)}, u32[]{:S(2)}) copy-start(bf16[9,512,256]{2,1,0:T(8,128)(2,1)S(1)} %get-tuple-element.26) | copy-start | bytes 7077892
  21.4 1.2 %copy-start.10 = (bf16[9,384,256]{2,1,0:T(8,128)(2,1)}, bf16[9,384,256]{2,1,0:T(8,128)(2,1)S(1)}, u32[]{:S(2)}) copy-start(bf16[9,384,256]{2,1,0:T(8,128)(2,1)S(1)} %get-tuple-element.23) | copy-start | bytes 5308420
  22.6 0.7 copy-start.14
  23.2 0.7 copy-start.16
  25.5 13.2 %collective-permute-start.5 = (bf16[4,48,128]{2,1,0:T(8,128)(2,1)S(1)}, bf16[4,48,128]{2,1,0:T(8,128)(2,1)S(1)}, u32[]{:S(2)}, u32[]{:S(2)}) collective-permute-start(bf16[4,48,128]{2,1,0:T(8,128)(2,1)S(1)} %shard_map.110.b2), channel_id=1, source_target_pairs={{0,192},{32,224},{64,0},{96,32},{128,64},{160,96},{192,128},{224,1... | collective-permute-start | bytes 147464 | tf_op jit(solution)/shard_map/ppermute | solution.py:14
  28.1 10.6 %collective-permute-start.4 = (bf16[4,48,128]{2,1,0:T(8,128)(2,1)S(1)}, bf16[4,48,128]{2,1,0:T(8,128)(2,1)S(1)}, u32[]{:S(2)}, u32[]{:S(2)}) collective-permute-start(bf16[4,48,128]{2,1,0:T(8,128)(2,1)S(1)} %shard_map.110.b2), channel_id=1, source_target_pairs={{0,224},{32,0},{64,32},{96,64},{128,96},{160,128},{192,160},{224,1... | collective-permute-start | bytes 147464 | tf_op jit(solution)/shard_map/ppermute | solution.py:14
  29.6 9.1 %collective-permute-start.3 = (bf16[4,48,128]{2,1,0:T(8,128)(2,1)S(1)}, bf16[4,48,128]{2,1,0:T(8,128)(2,1)S(1)}, u32[]{:S(2)}, u32[]{:S(2)}) collective-permute-start(bf16[4,48,128]{2,1,0:T(8,128)(2,1)S(1)} %shard_map.110.b2), channel_id=1, source_target_pairs={{0,32},{32,64},{64,96},{96,128},{128,160},{160,192},{192,224},{224... | collective-permute-start | bytes 147464 | tf_op jit(solution)/shard_map/ppermute | solution.py:14
  30.2 8.6 %collective-permute-start.2 = (bf16[4,48,128]{2,1,0:T(8,128)(2,1)S(1)}, bf16[4,48,128]{2,1,0:T(8,128)(2,1)S(1)}, u32[]{:S(2)}, u32[]{:S(2)}) collective-permute-start(bf16[4,48,128]{2,1,0:T(8,128)(2,1)S(1)} %shard_map.110.b2), channel_id=1, source_target_pairs={{0,64},{32,96},{64,128},{96,160},{128,192},{160,224},{192,0},{224,... | collective-permute-start | bytes 147464 | tf_op jit(solution)/shard_map/ppermute | solution.py:14
  38.9 11.9 %collective-permute-start.6 = (bf16[20,16,128]{2,1,0:T(8,128)(2,1)S(1)}, bf16[20,16,128]{2,1,0:T(8,128)(2,1)S(1)}, u32[]{:S(2)}, u32[]{:S(2)}) collective-permute-start(bf16[20,16,128]{2,1,0:T(8,128)(2,1)S(1)} %get-tuple-element.21), channel_id=1, source_target_pairs={{0,1},{1,2},{2,3},{3,4},{4,5},{5,6},{6,7},{7,0},{8,9},{9,10},{10,1... | collective-permute-start | bytes 245768 | tf_op jit(solution)/shard_map/ppermute | solution.py:14
  38.9 11.9 %collective-permute-start.7 = (bf16[20,16,128]{2,1,0:T(8,128)(2,1)S(1)}, bf16[20,16,128]{2,1,0:T(8,128)(2,1)S(1)}, u32[]{:S(2)}, u32[]{:S(2)}) collective-permute-start(bf16[20,16,128]{2,1,0:T(8,128)(2,1)S(1)} %get-tuple-element.22), channel_id=1, source_target_pairs={{0,7},{1,0},{2,1},{3,2},{4,3},{5,4},{6,5},{7,6},{8,15},{9,8},{10,9... | collective-permute-start | bytes 245768 | tf_op jit(solution)/shard_map/ppermute | solution.py:14
  41.9 1.5 %copy-start.11 = (bf16[9,384,256]{2,1,0:T(8,128)(2,1)S(1)}, bf16[9,384,256]{2,1,0:T(8,128)(2,1)}, u32[]{:S(2)}) copy-start(bf16[9,384,256]{2,1,0:T(8,128)(2,1)} %copy-done.10) | copy-start | bytes 5308420
  43.3 7.5 %copy-start.1 = (bf16[3,4,32,16]{2,3,1,0:T(8,128)(2,1)S(1)}, bf16[3,4,32,16]{2,3,1,0:T(8,128)(2,1)}, u32[]{:S(2)}) copy-start(bf16[3,4,32,16]{2,3,1,0:T(8,128)(2,1)} %param.11) | copy-start | bytes 36868
  43.3 7.5 %copy-start.9 = (bf16[9,512,256]{2,1,0:T(8,128)(2,1)S(1)}, bf16[9,512,256]{2,1,0:T(8,128)(2,1)}, u32[]{:S(2)}) copy-start(bf16[9,512,256]{2,1,0:T(8,128)(2,1)} %copy-done.8) | copy-start | bytes 7077892
  43.3 7.5 %copy-start.12 = (bf16[9,384,256]{2,1,0:T(8,128)(2,1)S(1)}, bf16[9,384,256]{2,1,0:T(8,128)(2,1)}, u32[]{:S(2)}) copy-start(bf16[9,384,256]{2,1,0:T(8,128)(2,1)} %copy-done.10) | copy-start | bytes 5308420
  43.3 7.5 %copy-start.15 = (bf16[512,128]{1,0:T(8,128)(2,1)S(1)}, bf16[512,128]{1,0:T(8,128)(2,1)}, u32[]{:S(2)}) copy-start(bf16[512,128]{1,0:T(8,128)(2,1)} %copy-done.14) | copy-start | bytes 393220
  43.4 7.5 %copy-start.17 = (bf16[128,512]{1,0:T(8,128)(2,1)S(1)}, bf16[128,512]{1,0:T(8,128)(2,1)}, u32[]{:S(2)}) copy-start(bf16[128,512]{1,0:T(8,128)(2,1)} %copy-done.16) | copy-start | bytes 393220

commit v2 on v1

v2 whole, which is shorter than its diff:
```python
import jax
import jax.numpy as jnp
import numpy as np
from jax import lax
from jax.experimental import pallas as pl
from jax.experimental.pallas import tpu as pltpu
from jax.sharding import PartitionSpec as P

BF, F32 = jnp.bfloat16, jnp.float32
ENC = ((0, 2), (2, 4), (4, 6), (6, 9))


def shift(block, axis, step):
    count = lax.axis_size(axis)
    return lax.ppermute(block, axis, [(i, (i + step) % count) for i in range(count)])


def act(value):
    return jnp.maximum(value, 0.1 * value)


def pick(quads):
    row = lax.broadcasted_iota(jnp.int32, (128, 128), 0)
    lane = lax.broadcasted_iota(jnp.int32, (128, 128), 1)
    slot, ch, zi = lane // 18, lane % 18 // 6, lane % 6
    columns = []
    for q in quads:
        z = 4 * q - 1 + zi
        start = jnp.where(z < 8, 48, jnp.where(z < 16, 16, jnp.where(z < 24, -16, 48)))
        hit = (row == start + 8 * ch + z) & (slot < 6) & (z >= 0) & (z < 32)
        columns.append(jnp.concatenate([jnp.where(hit & (slot % 3 == b), 1.0, 0.0).astype(BF) for b in range(3)], axis=0))
    return jnp.concatenate(columns, axis=1)


def lift_picker():
    table = np.zeros((2, 256, 2, 128), np.float32)
    for t in range(9):
        for ch in range(3):
            for zi in range(6):
                for zo in range(4):
                    if 0 <= zi - zo < 3:
                        r = 18 * t + 6 * ch + zi if t < 6 else 128 + 18 * (t - 6) + 6 * ch + zi
                        table[zo // 2, r, zo % 2, 32 * ch + 3 * t + zi - zo] = 1
    return table.reshape(2, 256, 256)


def banded_kernel(l_ref, h_ref, p_ref, e_hbm, m1_hbm, m2_hbm, u_hbm, j_hbm, wb, w1, w2, wu, wj, wh,
                  e_ref, m1_ref, m2_ref, u_ref, j_ref, sems):
    plan = ((e_hbm, e_ref), (j_hbm, j_ref), (m1_hbm, m1_ref), (m2_hbm, m2_ref), (u_hbm, u_ref))
    copies = [pltpu.make_async_copy(src, dst, sems.at[i]) for i, (src, dst) in enumerate(plan)]
    for copy in copies:
        copy.start()

    table = jnp.concatenate([jnp.concatenate([l_ref[k].astype(F32), jnp.zeros((5, 64), F32)], axis=0) for k in range(3)], axis=0)
    table = jnp.concatenate([table, jnp.zeros((32, 64), F32)], axis=0)
    zero = jnp.zeros_like(table)
    table = jnp.concatenate([jnp.concatenate([table, zero], axis=1), jnp.concatenate([zero, table], axis=1)], axis=0).astype(BF)
    for p in range(2):
        wb[2304 + 256 * p:2560 + 256 * p] = dot(p_ref[p], table).astype(BF)

    column = jnp.transpose(jnp.concatenate([h_ref[...].astype(F32), jnp.zeros((5, 64), F32)], axis=0))
    lane = lax.broadcasted_iota(jnp.int32, (64, 128), 1)
    spread = jnp.zeros((64, 128), F32)
    for k in range(3):
        spread = jnp.where(lane // 16 == k, column[:, k:k + 1], spread)
    for z in range(16):
        wh[64 * z:64 * z + 64] = jnp.where(lane % 16 == z, spread, 0.0).astype(BF)

    def turned(value):
        return jnp.transpose(value.astype(F32)).astype(BF)

    def step(t, carry):
        for raw in (e_ref, j_ref):
            c = [raw[3 * t + k] for k in range(3)]
            o = jnp.zeros_like(c[0])
            for k, pair in enumerate(((c[0], o), (c[1], c[0]), (c[2], c[1]), (o, c[2]))):
                block = turned(jnp.concatenate(pair, axis=0))
                if raw is e_ref:
                    wb[pl.ds(pl.multiple_of(256 * t + 64 * k, 64), 64), :] = block
                else:
                    wj[t, k] = block
        for raw, out in ((m1_ref, w1), (m2_ref, w2)):
            for k in range(3):
                out[t, k] = turned(raw[3 * t + k])
        return carry

    for copy in copies[:4]:
        copy.wait()
    lax.fori_loop(0, 9, step, 0)
    copies[4].wait()
    for k in range(4):
        wu[:, 128 * k:128 * k + 128] = turned(jnp.concatenate([u_ref[2 * k], u_ref[2 * k + 1]], axis=0))


def weights(lift, encode, down, m1, m2, up, decode, head):
    shapes = ((2816, 128), (9, 3, 128, 128), (9, 3, 128, 128), (128, 512), (9, 4, 128, 128), (1024, 128))
    raw = (encode, m1, m2, up, decode)
    wb, w1, w2, wu, wj, wh = call(
        banded_kernel, (jnp.transpose(lift, (2, 0, 1)), head, jnp.asarray(LIFT_PICK, BF), *raw),
        [VM] * 3 + [HBM] * 5, [(shape, BF) for shape in shapes],
        [V(w.shape, BF) for w in raw] + [pltpu.SemaphoreType.DMA((5,))], limit=PREP, flops=6_000_000_000,
    )
    return wb, jnp.swapaxes(down, 1, 2).reshape(512, 128), w1, w2, wu, wj, wh


def quad_rows(blocks):
    o = jnp.zeros_like(blocks[0])
    columns = [[blocks[z - 2 * p + 1] if 0 <= z - 2 * p + 1 < 4 else o for z in (0, 1, 2, 3, 4, -1)] for p in range(2)]
    return jnp.concatenate([jnp.concatenate(c, axis=0) for c in columns], axis=1)


def pair_rows(blocks):
    o = jnp.zeros_like(blocks[0])
    columns = [[blocks[z - p] if 0 <= z - p < 3 else o for z in range(4)] for p in range(2)]
    return jnp.concatenate([jnp.concatenate(c, axis=0) for c in columns], axis=1)


def dot(a, b):
    return jnp.dot(a, b, preferred_element_type=F32)


def rows(parts):
    flat = [p.reshape(-1, p.shape[-1]) for p in parts]
    return flat[0] if len(flat) == 1 else jnp.concatenate(flat, axis=1)


def up_one(v):
    return pltpu.roll(v, v.shape[-2] - 1, v.ndim - 2)


def plane_kernel(d_ref, a_ref, top_ref, low_ref):
    for x in range(4):
        parts = [d_ref[k, x].astype(F32)[h:h + 8] for h in (8, 0) for k in range(3)]
        t = jnp.transpose(jnp.concatenate(parts, axis=0))
        t = jnp.concatenate([t, jnp.zeros((32, 80), F32)], axis=1)
        a_ref[x] = t.astype(BF)
        top_ref[x] = t[24:].astype(BF)
        low_ref[x] = t[:8].astype(BF)


def join_kernel(before_ref, a_ref, after_ref, o_ref):
    for x in range(4):
        parts = [r[x].astype(F32) for r in (before_ref, a_ref, after_ref)]
        o_ref[x] = jnp.concatenate(parts, axis=0).astype(BF)


def rim_kernel(b0, b1, b2, b3, b4, left_ref, right_ref):
    lane = lax.broadcasted_iota(jnp.int32, (16, 128), 1)
    for x in range(20):
        own = (b0, b1, b2, b3, b4)[x // 4][x % 4].astype(F32)
        for out, first in ((left_ref, 0), (right_ref, 24)):
            g = [own[16 * k:16 * k + 16] for k in range(3)]
            g = [t if 24 * k == first else pltpu.roll(t, (24 * k - first) % 128, 1) for k, t in enumerate(g)]
            out[x] = jnp.where(lane < 24, g[0], jnp.where(lane < 48, g[1], g[2])).astype(BF)


def tiles(df, dt):
    for yo in range(8):
        for xo in range(12):
            t = [df[pl.ds((8 * xi + xo) * 48 + yo, 8, stride=6), :] for xi in range(2)]
            dt[yo, xo] = jnp.concatenate(t, axis=0).astype(BF)


def lift(dt, wb_ref, db, fp, pairs, count, index):
    for one, two in pairs:
        table = pick((one, two))
        r = dot(rows([dt[b:b + 6] for b in range(3)]), table)
        r = r.astype(BF).reshape(6, 12, 16, 256)
        db[one] = r[..., :128]
        db[two] = r[..., 128:]
    first_slots = lax.broadcasted_iota(jnp.int32, (16, 128), 1) < 54

    def step(i, carry):
        q = index(i)
        for g in range(2):
            y = slice(3 * g, 3 * g + 3)
            ta = jnp.where(first_slots, db[q, y, 0:10], db[q, y, 1:11])
            table = jnp.concatenate([wb_ref[2304:2560], wb_ref[2560:2816]], axis=1)
            r = act(dot(rows([ta, db[q, y, 2:12]]), table))
            for half in range(2):
                part = r[:, 128 * half:128 * half + 128].reshape(3, 10, 16, 128)
                fp[2 * q + half, y] = part.astype(BF)
                if g == 0:
                    low_rows = part[0:2].reshape(40, 8, 128)
                    fp[2 * q + half, 6:8] = up_one(low_rows).reshape(2, 10, 16, 128).astype(BF)
        return carry

    lax.fori_loop(0, count, step, 0)


def encode(fp, fe, wb_ref, sk, sd, base, count, index):
    low = lax.broadcasted_iota(jnp.int32, (16, 128), 1) < 64

    def edge_step(i, carry):
        q = index(i)
        fe[q] = jnp.where(low, fp[2 * q + 3], fp[2 * q])
        return carry

    lax.fori_loop(0, count, edge_step, 0)

    def step(i, carry):
        q = index(i)
        for g in range(2):
            y0 = 3 * g
            acc = None
            for lo, hi in ENC:
                parts = []
                for t in range(lo, hi):
                    a, b = t // 3, t % 3
                    sl = (slice(y0 + b, y0 + b + 3), slice(a, a + 8))
                    parts += [fp[(2 * q + 1,) + sl], fp[(2 * q + 2,) + sl], fe[(q,) + sl]]
                p = dot(rows(parts), jnp.concatenate([quad_rows([wb_ref[256 * t + 64 * k:256 * t + 64 * k + 64] for k in range(4)]) for t in range(lo, hi)], axis=0))
                acc = p if acc is None else acc + p
            r = act(acc).reshape(3, 8, 2, 8, 256)
            for half in range(2):
                part = r[..., 128 * half:128 * half + 128]
                packed = part.reshape(3, 8, 16, 128).astype(BF)
                sp = 2 * q + half - base
                for yy in range(3):
                    yo = y0 + yy
                    sk[sp, yo // 2, yo % 2] = packed[yy].reshape(4, 2, 16, 128)
                    mixed = [jnp.concatenate([part[yy, (5 + xo) % 8, (5 + xo) // 8], part[yy, (7 + xo) % 8, (7 + xo) // 8]], axis=0)
                             for xo in range(4)]
                    mixed = jnp.stack(mixed).reshape(8, 8, 128)
                    if yo == 5:
                        sd[sp, 0] = mixed.reshape(4, 16, 128).astype(BF)
                    moved = up_one(mixed)
                    sd[sp, yo + 1] = moved.reshape(4, 16, 128).astype(BF)
                    if yo == 0:
                        sd[sp, 7] = up_one(moved).reshape(4, 16, 128).astype(BF)
        return carry

    lax.fori_loop(0, count, step, 0)


def inner_kernel(b0, b1, b2, b3, b4, wb_ref, sk, sd, df, dt, db, fp, fe):
    for k, ref in enumerate((b0, b1, b2, b3, b4)):
        for x in range(4):
            df[192 * k + 48 * x:192 * k + 48 * x + 48] = ref[x].astype(F32)
    df[960:968] = jnp.zeros((8, 128), F32)
    tiles(df, dt)
    lift(dt, wb_ref, db, fp, ((2, 3), (4, 5)), 4, lambda i: i + 2)
    encode(fp, fe, wb_ref, sk, sd, 4, 3, lambda i: i + 2)


def outer_kernel(b0, b1, b2, b3, b4, left_ref, right_ref, x_ref, wb_ref,
                 wd_ref, w1_ref, w2_ref, wu_ref, wj_ref, wh_ref, sk_in, sd_in, o_ref,
                 df, dt, db, fp, fe, sk, sd, c1, c2, de, uu, es, eu, hs, ac, sems):
    plan = ((sk_in, sk.at[4:10]), (sd_in, sd.at[4:10]))
    copies = [pltpu.make_async_copy(src, dst, sems.at[i]) for i, (src, dst) in enumerate(plan)]
    for copy in copies:
        copy.start()

    lane = lax.broadcasted_iota(jnp.int32, (16, 128), 1)
    low = lane < 64
    for x in range(20):
        own = (b0, b1, b2, b3, b4)[x // 4][x % 4].astype(F32)
        left, right = left_ref[x].astype(F32), right_ref[x].astype(F32)
        for g in range(3):
            t = jnp.where(lane < 72, pltpu.roll(left, 48 - 24 * g if g < 2 else 0, 1) if g < 2 else left,
                          pltpu.roll(right, 72 - 24 * g, 1))
            df[48 * x + 16 * g:48 * x + 16 * g + 16] = jnp.where(lane < 48, own[16 * g:16 * g + 16], t)
    df[960:968] = jnp.zeros((8, 128), F32)
    tiles(df, dt)
    lift(dt, wb_ref, db, fp, ((0, 1), (2, 5), (6, 7)), 6, lambda i: i + 2 * (i // 3))
    encode(fp, fe, wb_ref, sk, sd, 0, 4, lambda i: i + 3 * (i // 2))

    for copy in copies:
        copy.wait()
    r = act(dot(rows([sk[:, :, b, :, a] for a in range(2) for b in range(2)]), wd_ref[...]))
    r = r.reshape(7, 2, 3, 4, 2, 8, 128)
    for yo in range(3):
        for xo in range(5):
            t = jnp.stack([r[:, :, yo, xo % 4, xo // 4], r[:, :, yo, (3 + xo) % 4, (3 + xo) // 4]], axis=2)
            c1[:, :, yo, xo] = t.reshape(7, 2, 16, 128).astype(BF)
            if yo < 2:
                c1[:, :, yo + 3, xo] = up_one(t.reshape(28, 8, 128)).reshape(7, 2, 16, 128).astype(BF)

    def middle(src, w_ref, zp, xn):
        m = zp * xn * 48
        ac[:m] = jnp.zeros((m, 256), F32)

        def tap(a, carry):
            parts, table = [], []
            for b in range(3):
                parts += [src[zi // 2:zi // 2 + zp, zi % 2, b:b + 3, pl.ds(a, xn)] for zi in range(4)]
                table.append(pair_rows([w_ref[3 * a + b, k] for k in range(3)]))
            ac[:m] += dot(rows(parts), jnp.concatenate(table, axis=0))
            return carry

        lax.fori_loop(0, 3, tap, 0)
        return act(ac[:m]).reshape(zp, 3, xn, 2, 8, 256)

    r = middle(c1, w1_ref, 6, 3)
    for half in range(2):
        part = r[..., 128 * half:128 * half + 128]
        for yo in range(3):
            for xo in range(4):
                t = jnp.stack([part[:, yo, xo % 3, xo // 3], part[:, yo, (2 + xo) % 3, (2 + xo) // 3]], axis=1)
                c2[:, half, yo, xo] = t.reshape(6, 16, 128).astype(BF)
                if yo < 2:
                    c2[:, half, yo + 3, xo] = up_one(t.reshape(12, 8, 128)).reshape(6, 16, 128).astype(BF)

    r = middle(c2, w2_ref, 5, 2).reshape(5, 3, 2, 16, 256).astype(BF)
    de[:, 0] = r[..., :128]
    de[:, 1] = r[..., 128:]

    r = act(dot(rows([de[...]]), wu_ref[...])).reshape(5, 2, 3, 2, 2, 8, 512)
    for yo in range(6):
        b = yo % 2
        for xo in range(4):
            t = []
            for f in (1 + xo, 3 + xo):
                a = f % 2
                n = 128 * (2 * a + b)
                t.append(r[:, :, yo // 2, (f // 2) % 2, f // 4, :, n:n + 128])
            t = jnp.stack(t, axis=2)
            if yo > 0:
                uu[:, :, yo - 1, xo] = t.reshape(5, 2, 16, 128).astype(BF)
            if yo < 3:
                uu[:, :, yo + 5, xo] = up_one(t.reshape(20, 8, 128)).reshape(5, 2, 16, 128).astype(BF)

    for q in range(4):
        es[q] = jnp.where(low, sd[2 * q + 5], sd[2 * q + 2])
        eu[q] = jnp.where(low, uu[q + 1, 1], uu[q, 0])

    if True:
        ac[:768] = jnp.zeros((768, 256), F32)

        def tap(a, carry):
            parts, table = [], []
            for b in range(3):
                ys, xs, t = slice(b, b + 6), pl.ds(a, 2), 3 * a + b
                own = [jnp.stack([sd[2 * q + 3 + k, ys, xs] for q in range(4)]) for k in range(2)]
                parts += own + [es[:, ys, xs], uu[0:4, 1, ys, xs], uu[1:5, 0, ys, xs], eu[:, ys, xs]]
                blocks = [wj_ref[t, k] for k in range(4)]
                table += [quad_rows([w[:64] for w in blocks]), quad_rows([w[64:] for w in blocks])]
            ac[:768] += dot(rows(parts), jnp.concatenate(table, axis=0))
            return carry

        lax.fori_loop(0, 3, tap, 0)
        acc = ac[:768]
        j = act(acc).astype(BF).reshape(4, 192, 256)
        h = dot(jnp.concatenate([j[q] for q in range(4)], axis=1), wh_ref[...]).reshape(6, 2, 2, 8, 128)
        for yo in range(6):
            for x in range(4):
                hs[pl.ds(48 * x + yo, 8, stride=6), :] = h[yo, x % 2, x // 2]
    for x in range(4):
        t = jnp.transpose(hs[48 * x:48 * x + 32, :])
        for k in range(3):
            o_ref[k, x] = t[16 * k:16 * k + 16] + x_ref[k, x].astype(F32)


VM = pl.BlockSpec(memory_space=pltpu.VMEM)
HBM = pl.BlockSpec(memory_space=pltpu.HBM)


def call(body, args, specs, shapes, scratch=(), limit=16, flops=1_000_000):
    many = isinstance(shapes, list)
    return pl.pallas_call(
        body,
        out_shape=[jax.ShapeDtypeStruct(*x) for x in shapes] if many else jax.ShapeDtypeStruct(*shapes),
        in_specs=specs,
        out_specs=[VM] * len(shapes) if many else VM,
        scratch_shapes=scratch,
        compiler_params=pltpu.CompilerParams(vmem_limit_bytes=limit << 20),
        cost_estimate=pl.CostEstimate(flops=flops, bytes_accessed=2_000_000, transcendentals=0),
    )(*args)


def planes(d):
    return call(plane_kernel, (d,), [VM], [((4, 32, 128), BF), ((4, 8, 128), BF), ((4, 8, 128), BF)])


def rims(blocks):
    return call(rim_kernel, blocks, [VM] * 5, [((20, 16, 128), BF)] * 2)


V = pltpu.VMEM
FIELDS = [V((968, 128), F32), V((8, 12, 16, 128), BF), V((8, 6, 12, 16, 128), BF), V((16, 8, 10, 16, 128), BF), V((7, 8, 10, 16, 128), BF)]
PREP, INNER, OUTER = 58, 20, 30
LIFT_PICK = lift_picker()


def inner(blocks, ws):
    args = (*blocks, ws[0])
    return call(
        inner_kernel, args, [VM] * 6, [((6, 3, 2, 4, 2, 16, 128), BF), ((6, 8, 4, 16, 128), BF)],
        FIELDS, limit=INNER, flops=8_000_000_000,
    )


def outer(blocks, left, right, d, ws, sk, sd):
    args = (*blocks, left, right, d, *ws, sk, sd)
    return call(
        outer_kernel, args, [VM] * 17, ((3, 4, 16, 32), F32),
        FIELDS + [
            V((14, 3, 2, 4, 2, 16, 128), BF), V((14, 8, 4, 16, 128), BF), V((7, 2, 5, 5, 16, 128), BF),
            V((6, 2, 5, 4, 16, 128), BF), V((5, 2, 3, 2, 16, 128), BF), V((5, 2, 8, 4, 16, 128), BF),
            V((4, 8, 4, 16, 128), BF), V((4, 8, 4, 16, 128), BF), V((192, 128), F32),
            V((864, 256), F32), pltpu.SemaphoreType.DMA((2,)),
        ], limit=OUTER, flops=16_000_000_000,
    )


def local(displacement, *raw):
    d = jnp.swapaxes(displacement, 2, 3)
    own, top, bottom = planes(d)
    before, after = shift(top, "gy", 1), shift(bottom, "gy", -1)
    ws = weights(*raw)
    block = call(join_kernel, (before, own, after), [VM] * 3, ((4, 48, 128), BF))
    blocks = (shift(block, "gx", 2), shift(block, "gx", 1), block, shift(block, "gx", -1), shift(block, "gx", -2))
    left, right = rims(blocks)
    left, right = shift(left, "gz", 1), shift(right, "gz", -1)
    sk, sd = inner(blocks, ws)
    return jnp.swapaxes(outer(blocks, left, right, d, ws, sk, sd), 2, 3)


def solution(mesh):
    placed = (P(None, "gx", "gy", "gz"), P(), P(), P(), P(), P(), P(), P(), P())
    return jax.shard_map(local, mesh=mesh, in_specs=placed, out_specs=P(None, "gx", "gy", "gz"), check_vma=False)
```

time: 76.6 us -> 57.8 us (0.75)
  local copies, waits for them, and re-layouts: 21 us -> 1.93 us
  waiting for transfers between devices: 0.02 us -> 3.01 us
  other arithmetic: 2.54 us -> 0 us
    unnamed x37 -> x18, local copies, waits for them, and re-layouts: 14.3 us -> 1.93 us
    reshape x4 -> x0, local copies, waits for them, and re-layouts: 4.27 us -> none  [the longest x2 3.49 us: head_matrix(): return jnp.pad(m.reshape(1024, 48), ((0, 0), (0, 80)))]
    ppermute x8, waiting for transfers between devices: 0.02 us -> 3.01 us  [shift(): lax.ppermute(block, axis, [(i, (i + step) % count) for i in range(count)])]
    pallas_call x1 -> x0, Pallas kernels: 2.25 us -> none  [weights(): pl.pallas_call(banded_kernel, out_shape=[jax.ShapeDtypeStruct(shape, BF)...]
    pallas_call x5 -> x6, Pallas kernels: 32.7 us -> 34.3 us  [call(): pl.pallas_call(body, out_shape=[jax.ShapeDtypeStruct(*x) for x in shapes]...]
    transpose x1 -> x0, other arithmetic: 1.47 us -> none  [head_matrix(): m = jnp.einsum('zs,ck->zcks', jnp.eye(16, dtype=BF), wt)]
    concatenate x2 -> x0, other arithmetic: 1.07 us -> none  [the longest x1 0.95 us: lift_matrix(): jnp.concatenate([m[:108], jnp.zeros((20, 256), BF), m[108:], jnp.zeros((7...]
    pad x1 -> x0, local copies, waits for them, and re-layouts: 1 us -> none  [head_matrix(): return jnp.pad(m.reshape(1024, 48), ((0, 0), (0, 80)))]
  transfers between devices with their start and end apart: 8 -> 8, of which waited for: 0 -> 2; matrix products, arithmetic and copies ran while one was open for 14% -> 0% of each run, Pallas kernels for 13% -> 24%
where the time goes in v2:
time: 57.8 us; the launch traced here: 56.7 us
  Pallas kernels  34.3 us (59%)
  starting transfers between devices  17.2 us (30%)
  waiting for transfers between devices  3.01 us (5%)
  local copies, waits for them, and re-layouts  1.93 us (3%)
    pallas_call x6, Pallas kernels, call(): pl.pallas_call(body, out_shape=[jax.ShapeDtypeStruct(*x) for x in shapes]...  34.3 us
    ppermute x8, starting transfers between devices, shift(): lax.ppermute(block, axis, [(i, (i + step) % count) for i in range(count)])  17.2 us
    ppermute x8, waiting for transfers between devices, shift(): lax.ppermute(block, axis, [(i, (i + step) % count) for i in range(count)])  3.01 us
    unnamed x18, local copies, waits for them, and re-layouts  1.93 us
  transfers between devices with their start and end apart: 8, of which 2 were waited for; matrix products, arithmetic and copies ran while one was open for 0% of the time, Pallas kernels for 24%

profile of v2, /device:TPU:2, one launch (start us, length us, event | category | flops | bytes accessed | tf_op | source)
XLA Modules:
  0.0 56.7 jit_solution(10615623801507517711)
XLA Ops:
  0.0 0.8 %copy-done = bf16[3,4,32,16]{2,3,1,0:T(8,128)(2,1)S(1)} copy-done((bf16[3,4,32,16]{2,3,1,0:T(8,128)(2,1)S(1)}, bf16[3,4,32,16]{2,3,1,0:T(8,128)(2,1)}, u32[]{:S(2)}) %copy-start) | copy-done | bytes 12312
  0.8 0.1 shard_map.100
  0.9 3.3 %collective-permute-start = (bf16[4,8,128]{2,1,0:T(8,128)(2,1)S(1)}, bf16[4,8,128]{2,1,0:T(8,128)(2,1)S(1)}, u32[]{:S(2)}, u32[]{:S(2)}) collective-permute-start(bf16[4,8,128]{2,1,0:T(8,128)(2,1)S(1)} %get-tuple-element.18), channel_id=1, source_target_pairs={{0,8},{8,16},{16,24},{24,0},{1,9},{9,17},{17,25},{25,1},{2,10},{10... | collective-permute-start | bytes 24584 | tf_op jit(solution)/shard_map/ppermute | solution.py:15
  4.2 3.1 %collective-permute-start.1 = (bf16[4,8,128]{2,1,0:T(8,128)(2,1)S(1)}, bf16[4,8,128]{2,1,0:T(8,128)(2,1)S(1)}, u32[]{:S(2)}, u32[]{:S(2)}) collective-permute-start(bf16[4,8,128]{2,1,0:T(8,128)(2,1)S(1)} %get-tuple-element.20), channel_id=1, source_target_pairs={{0,24},{8,0},{16,8},{24,16},{1,25},{9,1},{17,9},{25,17},{2,26},{10... | collective-permute-start | bytes 24584 | tf_op jit(solution)/shard_map/ppermute | solution.py:15
  7.4 1.5 %collective-permute-done.before_ref = bf16[4,8,128]{2,1,0:T(8,128)(2,1)S(1)} collective-permute-done((bf16[4,8,128]{2,1,0:T(8,128)(2,1)S(1)}, bf16[4,8,128]{2,1,0:T(8,128)(2,1)S(1)}, u32[]{:S(2)}, u32[]{:S(2)}) %collective-permute-start) | collective-permute-done | bytes 8224 | tf_op jit(solution)/shard_map/ppermute | solution.py:15
  8.9 1.4 %collective-permute-done.1.after_ref = bf16[4,8,128]{2,1,0:T(8,128)(2,1)S(1)} collective-permute-done((bf16[4,8,128]{2,1,0:T(8,128)(2,1)S(1)}, bf16[4,8,128]{2,1,0:T(8,128)(2,1)S(1)}, u32[]{:S(2)}, u32[]{:S(2)}) %collective-permute-start.1) | collective-permute-done | bytes 8224 | tf_op jit(solution)/shard_map/ppermute | solution.py:15
  10.4 2.7 %collective-permute-start.5 = (bf16[4,48,128]{2,1,0:T(8,128)(2,1)S(1)}, bf16[4,48,128]{2,1,0:T(8,128)(2,1)S(1)}, u32[]{:S(2)}, u32[]{:S(2)}) collective-permute-start(bf16[4,48,128]{2,1,0:T(8,128)(2,1)S(1)} %shard_map.101.b2), channel_id=1, source_target_pairs={{0,192},{32,224},{64,0},{96,32},{128,64},{160,96},{192,128},{224,1... | collective-permute-start | bytes 147464 | tf_op jit(solution)/shard_map/ppermute | solution.py:15
  13.0 1.4 %collective-permute-start.4 = (bf16[4,48,128]{2,1,0:T(8,128)(2,1)S(1)}, bf16[4,48,128]{2,1,0:T(8,128)(2,1)S(1)}, u32[]{:S(2)}, u32[]{:S(2)}) collective-permute-start(bf16[4,48,128]{2,1,0:T(8,128)(2,1)S(1)} %shard_map.101.b2), channel_id=1, source_target_pairs={{0,224},{32,0},{64,32},{96,64},{128,96},{160,128},{192,160},{224,1... | collective-permute-start | bytes 147464 | tf_op jit(solution)/shard_map/ppermute | solution.py:15
  14.4 0.6 %collective-permute-start.3 = (bf16[4,48,128]{2,1,0:T(8,128)(2,1)S(1)}, bf16[4,48,128]{2,1,0:T(8,128)(2,1)S(1)}, u32[]{:S(2)}, u32[]{:S(2)}) collective-permute-start(bf16[4,48,128]{2,1,0:T(8,128)(2,1)S(1)} %shard_map.101.b2), channel_id=1, source_target_pairs={{0,32},{32,64},{64,96},{96,128},{128,160},{160,192},{192,224},{224... | collective-permute-start | bytes 147464 | tf_op jit(solution)/shard_map/ppermute | solution.py:15
  15.0 3.1 %collective-permute-start.2 = (bf16[4,48,128]{2,1,0:T(8,128)(2,1)S(1)}, bf16[4,48,128]{2,1,0:T(8,128)(2,1)S(1)}, u32[]{:S(2)}, u32[]{:S(2)}) collective-permute-start(bf16[4,48,128]{2,1,0:T(8,128)(2,1)S(1)} %shard_map.101.b2), channel_id=1, source_target_pairs={{0,64},{32,96},{64,128},{96,160},{128,192},{160,224},{192,0},{224,... | collective-permute-start | bytes 147464 | tf_op jit(solution)/shard_map/ppermute | solution.py:15
  18.1 6.5 %shard_map.103 = (bf16[2816,128]{1,0:T(8,128)(2,1)}, bf16[9,3,128,128]{3,2,1,0:T(8,128)(2,1)}, bf16[9,3,128,128]{3,2,1,0:T(8,128)(2,1)}, bf16[128,512]{1,0:T(8,1...) custom-call(bf16[3,27,64]{2,1,0:T(8,128)(2,1)} %bitcast.9, bf16[3,64]{1,0:T(4,128)(2,1)} %h_ref.1, ...), custom_call_target="tpu_custom_call" | custom-call | flops 6000000000 | bytes 2000000 | tf_op jit(solution)/shard_map/pallas_call | solution.py:360
  24.6 0.0 collective-permute-done.5.b4
  24.6 0.0 collective-permute-done.4.b3
  24.7 0.0 collective-permute-done.3.b1
  24.7 0.0 collective-permute-done.2.b0
  24.7 0.2 shard_map.102
  24.8 0.0 collective-permute-start.6
  24.9 2.9 %collective-permute-start.7 = (bf16[20,16,128]{2,1,0:T(8,128)(2,1)S(1)}, bf16[20,16,128]{2,1,0:T(8,128)(2,1)S(1)}, u32[]{:S(2)}, u32[]{:S(2)}) collective-permute-start(bf16[20,16,128]{2,1,0:T(8,128)(2,1)S(1)} %get-tuple-element.22), channel_id=1, source_target_pairs={{0,7},{1,0},{2,1},{3,2},{4,3},{5,4},{6,5},{7,6},{8,15},{9,8},{10,9... | collective-permute-start | bytes 245768 | tf_op jit(solution)/shard_map/ppermute | solution.py:15
  27.8 1.1 %copy-done.6 = bf16[2816,128]{1,0:T(8,128)(2,1)S(1)} copy-done((bf16[2816,128]{1,0:T(8,128)(2,1)S(1)}, bf16[2816,128]{1,0:T(8,128)(2,1)}, u32[]{:S(2)}) %copy-start.6) | copy-done | bytes 720920
  28.9 0.0 copy-start.5
  28.9 0.0 copy-start.7
  28.9 0.0 copy-start.8
  29.0 7.2 %shard_map.104 = (bf16[6,3,2,4,2,16,128]{6,5,4,3,2,1,0:T(8,128)(2,1)S(1)}, bf16[6,8,4,16,128]{4,3,2,1,0:T(8,128)(2,1)S(1)}) custom-call(bf16[4,48,128]{2,1,0:T(8,128)(2,1)S(1)} %collective-permute-done.2.b0, bf16[4,48,128]{2,1,0:T(8,128)(2,1)S(1)} %collective-permute-done.3.b1, bf16[4,48,128]{2,1,0:T(8,128)(2,1)S(1)} %shard_map.101.b2, ...), custom_call_target="tpu_custom_call" | custom-call | flops 8000000000 | bytes 2000000 | tf_op jit(solution)/shard_map/pallas_call | solution.py:360
  36.2 0.0 collective-permute-done.6.left_ref
  36.2 0.0 collective-permute-done.7.right_ref
  36.2 0.0 copy-done.1
  36.2 0.0 copy-done.2
  36.2 0.0 copy-done.3
  36.2 0.0 copy-done.4
  36.2 0.0 copy-done.5
  36.2 0.0 copy-done.7
  36.3 20.3 %shard_map.105 = f32[3,4,16,32]{3,2,1,0:T(8,128)} custom-call(bf16[4,48,128]{2,1,0:T(8,128)(2,1)S(1)} %collective-permute-done.2.b0, bf16[4,48,128]{2,1,0:T(8,128)(2,1)S(1)} %collective-permute-done.3.b1, bf16[4,48,128]{2,1,0:T(8,128)(2,1)S(1)} %shard_map.101.b2, bf16[4,48,128]{2,1,0:T(8,128)(2,1)S(1)} %collective-permute-done.4.b3, ...), custom_call_target="tpu_custom_call" | custom-call | flops 16000000000 | bytes 2000000 | tf_op jit(solution)/shard_map/pallas_call | solution.py:360
  (8 shorter events, 0.0 us)
Async XLA Ops:
  0.0 0.8 %copy-start = (bf16[3,4,32,16]{2,3,1,0:T(8,128)(2,1)S(1)}, bf16[3,4,32,16]{2,3,1,0:T(8,128)(2,1)}, u32[]{:S(2)}) copy-start(bf16[3,4,32,16]{2,3,1,0:T(8,128)(2,1)} %param.10) | copy-start | bytes 36868
  0.9 8.0 %collective-permute-start = (bf16[4,8,128]{2,1,0:T(8,128)(2,1)S(1)}, bf16[4,8,128]{2,1,0:T(8,128)(2,1)S(1)}, u32[]{:S(2)}, u32[]{:S(2)}) collective-permute-start(bf16[4,8,128]{2,1,0:T(8,128)(2,1)S(1)} %get-tuple-element.18), channel_id=1, source_target_pairs={{0,8},{8,16},{16,24},{24,0},{1,9},{9,17},{17,25},{25,1},{2,10},{10... | collective-permute-start | bytes 24584 | tf_op jit(solution)/shard_map/ppermute | solution.py:15
  4.2 6.1 %collective-permute-start.1 = (bf16[4,8,128]{2,1,0:T(8,128)(2,1)S(1)}, bf16[4,8,128]{2,1,0:T(8,128)(2,1)S(1)}, u32[]{:S(2)}, u32[]{:S(2)}) collective-permute-start(bf16[4,8,128]{2,1,0:T(8,128)(2,1)S(1)} %get-tuple-element.20), channel_id=1, source_target_pairs={{0,24},{8,0},{16,8},{24,16},{1,25},{9,1},{17,9},{25,17},{2,26},{10... | collective-permute-start | bytes 24584 | tf_op jit(solution)/shard_map/ppermute | solution.py:15
  10.4 14.3 %collective-permute-start.5 = (bf16[4,48,128]{2,1,0:T(8,128)(2,1)S(1)}, bf16[4,48,128]{2,1,0:T(8,128)(2,1)S(1)}, u32[]{:S(2)}, u32[]{:S(2)}) collective-permute-start(bf16[4,48,128]{2,1,0:T(8,128)(2,1)S(1)} %shard_map.101.b2), channel_id=1, source_target_pairs={{0,192},{32,224},{64,0},{96,32},{128,64},{160,96},{192,128},{224,1... | collective-permute-start | bytes 147464 | tf_op jit(solution)/shard_map/ppermute | solution.py:15
  13.0 11.6 %collective-permute-start.4 = (bf16[4,48,128]{2,1,0:T(8,128)(2,1)S(1)}, bf16[4,48,128]{2,1,0:T(8,128)(2,1)S(1)}, u32[]{:S(2)}, u32[]{:S(2)}) collective-permute-start(bf16[4,48,128]{2,1,0:T(8,128)(2,1)S(1)} %shard_map.101.b2), channel_id=1, source_target_pairs={{0,224},{32,0},{64,32},{96,64},{128,96},{160,128},{192,160},{224,1... | collective-permute-start | bytes 147464 | tf_op jit(solution)/shard_map/ppermute | solution.py:15
  14.4 10.2 %collective-permute-start.3 = (bf16[4,48,128]{2,1,0:T(8,128)(2,1)S(1)}, bf16[4,48,128]{2,1,0:T(8,128)(2,1)S(1)}, u32[]{:S(2)}, u32[]{:S(2)}) collective-permute-start(bf16[4,48,128]{2,1,0:T(8,128)(2,1)S(1)} %shard_map.101.b2), channel_id=1, source_target_pairs={{0,32},{32,64},{64,96},{96,128},{128,160},{160,192},{192,224},{224... | collective-permute-start | bytes 147464 | tf_op jit(solution)/shard_map/ppermute | solution.py:15
  15.0 9.6 %collective-permute-start.2 = (bf16[4,48,128]{2,1,0:T(8,128)(2,1)S(1)}, bf16[4,48,128]{2,1,0:T(8,128)(2,1)S(1)}, u32[]{:S(2)}, u32[]{:S(2)}) collective-permute-start(bf16[4,48,128]{2,1,0:T(8,128)(2,1)S(1)} %shard_map.101.b2), channel_id=1, source_target_pairs={{0,64},{32,96},{64,128},{96,160},{128,192},{160,224},{192,0},{224,... | collective-permute-start | bytes 147464 | tf_op jit(solution)/shard_map/ppermute | solution.py:15
  24.8 11.3 %collective-permute-start.6 = (bf16[20,16,128]{2,1,0:T(8,128)(2,1)S(1)}, bf16[20,16,128]{2,1,0:T(8,128)(2,1)S(1)}, u32[]{:S(2)}, u32[]{:S(2)}) collective-permute-start(bf16[20,16,128]{2,1,0:T(8,128)(2,1)S(1)} %get-tuple-element.21), channel_id=1, source_target_pairs={{0,1},{1,2},{2,3},{3,4},{4,5},{5,6},{6,7},{7,0},{8,9},{9,10},{10,1... | collective-permute-start | bytes 245768 | tf_op jit(solution)/shard_map/ppermute | solution.py:15
  24.9 11.3 %collective-permute-start.7 = (bf16[20,16,128]{2,1,0:T(8,128)(2,1)S(1)}, bf16[20,16,128]{2,1,0:T(8,128)(2,1)S(1)}, u32[]{:S(2)}, u32[]{:S(2)}) collective-permute-start(bf16[20,16,128]{2,1,0:T(8,128)(2,1)S(1)} %get-tuple-element.22), channel_id=1, source_target_pairs={{0,7},{1,0},{2,1},{3,2},{4,3},{5,4},{6,5},{7,6},{8,15},{9,8},{10,9... | collective-permute-start | bytes 245768 | tf_op jit(solution)/shard_map/ppermute | solution.py:15
  27.8 1.1 %copy-start.6 = (bf16[2816,128]{1,0:T(8,128)(2,1)S(1)}, bf16[2816,128]{1,0:T(8,128)(2,1)}, u32[]{:S(2)}) copy-start(bf16[2816,128]{1,0:T(8,128)(2,1)} %get-tuple-element.23.wb_ref) | copy-start | bytes 2162692
  28.9 7.3 %copy-start.1 = (bf16[3,4,32,16]{2,3,1,0:T(8,128)(2,1)S(1)}, bf16[3,4,32,16]{2,3,1,0:T(8,128)(2,1)}, u32[]{:S(2)}) copy-start(bf16[3,4,32,16]{2,3,1,0:T(8,128)(2,1)} %param.10) | copy-start | bytes 36868
  28.9 7.3 %copy-start.2 = (bf16[8,128,64]{1,2,0:T(8,128)(2,1)S(1)}, bf16[8,128,64]{1,2,0:T(8,128)(2,1)}, u32[]{:S(2)}) copy-start(bf16[8,128,64]{1,2,0:T(8,128)(2,1)} %param.13) | copy-start | bytes 393220
  28.9 7.3 %copy-start.3 = (bf16[9,4,128,128]{3,2,1,0:T(8,128)(2,1)S(1)}, bf16[9,4,128,128]{3,2,1,0:T(8,128)(2,1)}, u32[]{:S(2)}) copy-start(bf16[9,4,128,128]{3,2,1,0:T(8,128)(2,1)} %get-tuple-element.27.wj_ref) | copy-start | bytes 3538948
  28.9 7.3 %copy-start.4 = (bf16[9,3,128,128]{3,2,1,0:T(8,128)(2,1)S(1)}, bf16[9,3,128,128]{3,2,1,0:T(8,128)(2,1)}, u32[]{:S(2)}) copy-start(bf16[9,3,128,128]{3,2,1,0:T(8,128)(2,1)} %get-tuple-element.24.w1_ref) | copy-start | bytes 2654212
  28.9 7.3 %copy-start.5 = (bf16[9,3,128,128]{3,2,1,0:T(8,128)(2,1)S(1)}, bf16[9,3,128,128]{3,2,1,0:T(8,128)(2,1)}, u32[]{:S(2)}) copy-start(bf16[9,3,128,128]{3,2,1,0:T(8,128)(2,1)} %get-tuple-element.25.w2_ref) | copy-start | bytes 2654212
  28.9 7.3 %copy-start.7 = (bf16[1024,128]{1,0:T(8,128)(2,1)S(1)}, bf16[1024,128]{1,0:T(8,128)(2,1)}, u32[]{:S(2)}) copy-start(bf16[1024,128]{1,0:T(8,128)(2,1)} %get-tuple-element.28.wh_ref) | copy-start | bytes 786436
  28.9 7.3 %copy-start.8 = (bf16[128,512]{1,0:T(8,128)(2,1)S(1)}, bf16[128,512]{1,0:T(8,128)(2,1)}, u32[]{:S(2)}) copy-start(bf16[128,512]{1,0:T(8,128)(2,1)} %get-tuple-element.26.wu_ref) | copy-start | bytes 393220

commit v3 on v2

--- a/solution.py
+++ b/solution.py
@@ -373,7 +373,7 @@
 
 
 def rims(blocks):
-    return call(rim_kernel, blocks, [VM] * 5, [((20, 16, 128), BF)] * 2)
+    return call(rim_kernel, blocks, [VM] * 5, [((20, 16, 128), BF)] * 2, flops=4_000_000_000)
 
 
 V = pltpu.VMEM

time: 57.8 us -> 56.7 us (0.981)
  local copies, waits for them, and re-layouts: 1.93 us -> 0.83 us
    unnamed x18, local copies, waits for them, and re-layouts: 1.93 us -> 0.83 us
  transfers between devices with their start and end apart: 8 -> 8, of which waited for: 2 -> 2; matrix products, arithmetic and copies ran while one was open for 0% -> 0% of each run, Pallas kernels for 24% -> 25%
where the time goes in v3:
time: 56.7 us; the launch traced here: 55.6 us
  Pallas kernels  34.3 us (60%)
  starting transfers between devices  17.2 us (30%)
  waiting for transfers between devices  3.01 us (5%)
  local copies, waits for them, and re-layouts  0.83 us (1%)
    pallas_call x6, Pallas kernels, call(): pl.pallas_call(body, out_shape=[jax.ShapeDtypeStruct(*x) for x in shapes]...  34.3 us
    ppermute x8, starting transfers between devices, shift(): lax.ppermute(block, axis, [(i, (i + step) % count) for i in range(count)])  17.2 us
    ppermute x8, waiting for transfers between devices, shift(): lax.ppermute(block, axis, [(i, (i + step) % count) for i in range(count)])  3.01 us
  transfers between devices with their start and end apart: 8, of which 2 were waited for; matrix products, arithmetic and copies ran while one was open for 0% of the time, Pallas kernels for 25%

profile of v3, /device:TPU:2, one launch (start us, length us, event | category | flops | bytes accessed | tf_op | source)
XLA Modules:
  0.0 55.6 jit_solution(8404775038708688279)
XLA Ops:
  0.0 0.8 %copy-done = bf16[3,4,32,16]{2,3,1,0:T(8,128)(2,1)S(1)} copy-done((bf16[3,4,32,16]{2,3,1,0:T(8,128)(2,1)S(1)}, bf16[3,4,32,16]{2,3,1,0:T(8,128)(2,1)}, u32[]{:S(2)}) %copy-start) | copy-done | bytes 12312
  0.8 0.1 shard_map.100
  0.9 3.3 %collective-permute-start = (bf16[4,8,128]{2,1,0:T(8,128)(2,1)S(1)}, bf16[4,8,128]{2,1,0:T(8,128)(2,1)S(1)}, u32[]{:S(2)}, u32[]{:S(2)}) collective-permute-start(bf16[4,8,128]{2,1,0:T(8,128)(2,1)S(1)} %get-tuple-element.18), channel_id=1, source_target_pairs={{0,8},{8,16},{16,24},{24,0},{1,9},{9,17},{17,25},{25,1},{2,10},{10... | collective-permute-start | bytes 24584 | tf_op jit(solution)/shard_map/ppermute | solution.py:15
  4.2 3.1 %collective-permute-start.1 = (bf16[4,8,128]{2,1,0:T(8,128)(2,1)S(1)}, bf16[4,8,128]{2,1,0:T(8,128)(2,1)S(1)}, u32[]{:S(2)}, u32[]{:S(2)}) collective-permute-start(bf16[4,8,128]{2,1,0:T(8,128)(2,1)S(1)} %get-tuple-element.20), channel_id=1, source_target_pairs={{0,24},{8,0},{16,8},{24,16},{1,25},{9,1},{17,9},{25,17},{2,26},{10... | collective-permute-start | bytes 24584 | tf_op jit(solution)/shard_map/ppermute | solution.py:15
  7.4 1.5 %collective-permute-done.before_ref = bf16[4,8,128]{2,1,0:T(8,128)(2,1)S(1)} collective-permute-done((bf16[4,8,128]{2,1,0:T(8,128)(2,1)S(1)}, bf16[4,8,128]{2,1,0:T(8,128)(2,1)S(1)}, u32[]{:S(2)}, u32[]{:S(2)}) %collective-permute-start) | collective-permute-done | bytes 8224 | tf_op jit(solution)/shard_map/ppermute | solution.py:15
  8.9 1.4 %collective-permute-done.1.after_ref = bf16[4,8,128]{2,1,0:T(8,128)(2,1)S(1)} collective-permute-done((bf16[4,8,128]{2,1,0:T(8,128)(2,1)S(1)}, bf16[4,8,128]{2,1,0:T(8,128)(2,1)S(1)}, u32[]{:S(2)}, u32[]{:S(2)}) %collective-permute-start.1) | collective-permute-done | bytes 8224 | tf_op jit(solution)/shard_map/ppermute | solution.py:15
  10.4 2.7 %collective-permute-start.5 = (bf16[4,48,128]{2,1,0:T(8,128)(2,1)S(1)}, bf16[4,48,128]{2,1,0:T(8,128)(2,1)S(1)}, u32[]{:S(2)}, u32[]{:S(2)}) collective-permute-start(bf16[4,48,128]{2,1,0:T(8,128)(2,1)S(1)} %shard_map.101.b2), channel_id=1, source_target_pairs={{0,192},{32,224},{64,0},{96,32},{128,64},{160,96},{192,128},{224,1... | collective-permute-start | bytes 147464 | tf_op jit(solution)/shard_map/ppermute | solution.py:15
  13.0 1.4 %collective-permute-start.4 = (bf16[4,48,128]{2,1,0:T(8,128)(2,1)S(1)}, bf16[4,48,128]{2,1,0:T(8,128)(2,1)S(1)}, u32[]{:S(2)}, u32[]{:S(2)}) collective-permute-start(bf16[4,48,128]{2,1,0:T(8,128)(2,1)S(1)} %shard_map.101.b2), channel_id=1, source_target_pairs={{0,224},{32,0},{64,32},{96,64},{128,96},{160,128},{192,160},{224,1... | collective-permute-start | bytes 147464 | tf_op jit(solution)/shard_map/ppermute | solution.py:15
  14.4 0.6 %collective-permute-start.3 = (bf16[4,48,128]{2,1,0:T(8,128)(2,1)S(1)}, bf16[4,48,128]{2,1,0:T(8,128)(2,1)S(1)}, u32[]{:S(2)}, u32[]{:S(2)}) collective-permute-start(bf16[4,48,128]{2,1,0:T(8,128)(2,1)S(1)} %shard_map.101.b2), channel_id=1, source_target_pairs={{0,32},{32,64},{64,96},{96,128},{128,160},{160,192},{192,224},{224... | collective-permute-start | bytes 147464 | tf_op jit(solution)/shard_map/ppermute | solution.py:15
  15.0 3.1 %collective-permute-start.2 = (bf16[4,48,128]{2,1,0:T(8,128)(2,1)S(1)}, bf16[4,48,128]{2,1,0:T(8,128)(2,1)S(1)}, u32[]{:S(2)}, u32[]{:S(2)}) collective-permute-start(bf16[4,48,128]{2,1,0:T(8,128)(2,1)S(1)} %shard_map.101.b2), channel_id=1, source_target_pairs={{0,64},{32,96},{64,128},{96,160},{128,192},{160,224},{192,0},{224,... | collective-permute-start | bytes 147464 | tf_op jit(solution)/shard_map/ppermute | solution.py:15
  18.1 6.5 %shard_map.103 = (bf16[2816,128]{1,0:T(8,128)(2,1)}, bf16[9,3,128,128]{3,2,1,0:T(8,128)(2,1)}, bf16[9,3,128,128]{3,2,1,0:T(8,128)(2,1)}, bf16[128,512]{1,0:T(8,1...) custom-call(bf16[3,27,64]{2,1,0:T(8,128)(2,1)} %bitcast.9, bf16[3,64]{1,0:T(4,128)(2,1)} %h_ref.1, ...), custom_call_target="tpu_custom_call" | custom-call | flops 6000000000 | bytes 2000000 | tf_op jit(solution)/shard_map/pallas_call | solution.py:360
  24.6 0.0 copy-start.6
  24.6 0.0 collective-permute-done.5.b4
  24.7 0.0 collective-permute-done.4.b3
  24.7 0.0 collective-permute-done.3.b1
  24.7 0.0 collective-permute-done.2.b0
  24.7 0.2 shard_map.102
  24.8 0.0 collective-permute-start.6
  24.9 2.9 %collective-permute-start.7 = (bf16[20,16,128]{2,1,0:T(8,128)(2,1)S(1)}, bf16[20,16,128]{2,1,0:T(8,128)(2,1)S(1)}, u32[]{:S(2)}, u32[]{:S(2)}) collective-permute-start(bf16[20,16,128]{2,1,0:T(8,128)(2,1)S(1)} %get-tuple-element.22), channel_id=1, source_target_pairs={{0,7},{1,0},{2,1},{3,2},{4,3},{5,4},{6,5},{7,6},{8,15},{9,8},{10,9... | collective-permute-start | bytes 245768 | tf_op jit(solution)/shard_map/ppermute | solution.py:15
  27.8 0.0 copy-done.6
  27.8 0.0 copy-start.4
  27.8 0.0 copy-start.5
  27.8 0.0 copy-start.7
  27.9 0.0 copy-start.8
  27.9 7.2 %shard_map.104 = (bf16[6,3,2,4,2,16,128]{6,5,4,3,2,1,0:T(8,128)(2,1)S(1)}, bf16[6,8,4,16,128]{4,3,2,1,0:T(8,128)(2,1)S(1)}) custom-call(bf16[4,48,128]{2,1,0:T(8,128)(2,1)S(1)} %collective-permute-done.2.b0, bf16[4,48,128]{2,1,0:T(8,128)(2,1)S(1)} %collective-permute-done.3.b1, bf16[4,48,128]{2,1,0:T(8,128)(2,1)S(1)} %shard_map.101.b2, ...), custom_call_target="tpu_custom_call" | custom-call | flops 8000000000 | bytes 2000000 | tf_op jit(solution)/shard_map/pallas_call | solution.py:360
  35.1 0.0 collective-permute-done.6.left_ref
  35.1 0.0 collective-permute-done.7.right_ref
  35.1 0.0 copy-done.1
  35.1 0.0 copy-done.2
  35.1 0.0 copy-done.3
  35.1 0.0 copy-done.4
  35.2 20.3 %shard_map.105 = f32[3,4,16,32]{3,2,1,0:T(8,128)} custom-call(bf16[4,48,128]{2,1,0:T(8,128)(2,1)S(1)} %collective-permute-done.2.b0, bf16[4,48,128]{2,1,0:T(8,128)(2,1)S(1)} %collective-permute-done.3.b1, bf16[4,48,128]{2,1,0:T(8,128)(2,1)S(1)} %shard_map.101.b2, bf16[4,48,128]{2,1,0:T(8,128)(2,1)S(1)} %collective-permute-done.4.b3, ...), custom_call_target="tpu_custom_call" | custom-call | flops 16000000000 | bytes 2000000 | tf_op jit(solution)/shard_map/pallas_call | solution.py:360
  (8 shorter events, 0.0 us)
Async XLA Ops:
  0.0 0.8 %copy-start = (bf16[3,4,32,16]{2,3,1,0:T(8,128)(2,1)S(1)}, bf16[3,4,32,16]{2,3,1,0:T(8,128)(2,1)}, u32[]{:S(2)}) copy-start(bf16[3,4,32,16]{2,3,1,0:T(8,128)(2,1)} %param.10) | copy-start | bytes 36868
  0.9 8.0 %collective-permute-start = (bf16[4,8,128]{2,1,0:T(8,128)(2,1)S(1)}, bf16[4,8,128]{2,1,0:T(8,128)(2,1)S(1)}, u32[]{:S(2)}, u32[]{:S(2)}) collective-permute-start(bf16[4,8,128]{2,1,0:T(8,128)(2,1)S(1)} %get-tuple-element.18), channel_id=1, source_target_pairs={{0,8},{8,16},{16,24},{24,0},{1,9},{9,17},{17,25},{25,1},{2,10},{10... | collective-permute-start | bytes 24584 | tf_op jit(solution)/shard_map/ppermute | solution.py:15
  4.2 6.1 %collective-permute-start.1 = (bf16[4,8,128]{2,1,0:T(8,128)(2,1)S(1)}, bf16[4,8,128]{2,1,0:T(8,128)(2,1)S(1)}, u32[]{:S(2)}, u32[]{:S(2)}) collective-permute-start(bf16[4,8,128]{2,1,0:T(8,128)(2,1)S(1)} %get-tuple-element.20), channel_id=1, source_target_pairs={{0,24},{8,0},{16,8},{24,16},{1,25},{9,1},{17,9},{25,17},{2,26},{10... | collective-permute-start | bytes 24584 | tf_op jit(solution)/shard_map/ppermute | solution.py:15
  10.4 14.3 %collective-permute-start.5 = (bf16[4,48,128]{2,1,0:T(8,128)(2,1)S(1)}, bf16[4,48,128]{2,1,0:T(8,128)(2,1)S(1)}, u32[]{:S(2)}, u32[]{:S(2)}) collective-permute-start(bf16[4,48,128]{2,1,0:T(8,128)(2,1)S(1)} %shard_map.101.b2), channel_id=1, source_target_pairs={{0,192},{32,224},{64,0},{96,32},{128,64},{160,96},{192,128},{224,1... | collective-permute-start | bytes 147464 | tf_op jit(solution)/shard_map/ppermute | solution.py:15
  13.0 11.6 %collective-permute-start.4 = (bf16[4,48,128]{2,1,0:T(8,128)(2,1)S(1)}, bf16[4,48,128]{2,1,0:T(8,128)(2,1)S(1)}, u32[]{:S(2)}, u32[]{:S(2)}) collective-permute-start(bf16[4,48,128]{2,1,0:T(8,128)(2,1)S(1)} %shard_map.101.b2), channel_id=1, source_target_pairs={{0,224},{32,0},{64,32},{96,64},{128,96},{160,128},{192,160},{224,1... | collective-permute-start | bytes 147464 | tf_op jit(solution)/shard_map/ppermute | solution.py:15
  14.4 10.2 %collective-permute-start.3 = (bf16[4,48,128]{2,1,0:T(8,128)(2,1)S(1)}, bf16[4,48,128]{2,1,0:T(8,128)(2,1)S(1)}, u32[]{:S(2)}, u32[]{:S(2)}) collective-permute-start(bf16[4,48,128]{2,1,0:T(8,128)(2,1)S(1)} %shard_map.101.b2), channel_id=1, source_target_pairs={{0,32},{32,64},{64,96},{96,128},{128,160},{160,192},{192,224},{224... | collective-permute-start | bytes 147464 | tf_op jit(solution)/shard_map/ppermute | solution.py:15
  15.0 9.6 %collective-permute-start.2 = (bf16[4,48,128]{2,1,0:T(8,128)(2,1)S(1)}, bf16[4,48,128]{2,1,0:T(8,128)(2,1)S(1)}, u32[]{:S(2)}, u32[]{:S(2)}) collective-permute-start(bf16[4,48,128]{2,1,0:T(8,128)(2,1)S(1)} %shard_map.101.b2), channel_id=1, source_target_pairs={{0,64},{32,96},{64,128},{96,160},{128,192},{160,224},{192,0},{224,... | collective-permute-start | bytes 147464 | tf_op jit(solution)/shard_map/ppermute | solution.py:15
  24.6 3.2 %copy-start.6 = (bf16[2816,128]{1,0:T(8,128)(2,1)S(1)}, bf16[2816,128]{1,0:T(8,128)(2,1)}, u32[]{:S(2)}) copy-start(bf16[2816,128]{1,0:T(8,128)(2,1)} %get-tuple-element.23.wb_ref) | copy-start | bytes 2162692
  24.8 10.2 %collective-permute-start.6 = (bf16[20,16,128]{2,1,0:T(8,128)(2,1)S(1)}, bf16[20,16,128]{2,1,0:T(8,128)(2,1)S(1)}, u32[]{:S(2)}, u32[]{:S(2)}) collective-permute-start(bf16[20,16,128]{2,1,0:T(8,128)(2,1)S(1)} %get-tuple-element.21), channel_id=1, source_target_pairs={{0,1},{1,2},{2,3},{3,4},{4,5},{5,6},{6,7},{7,0},{8,9},{9,10},{10,1... | collective-permute-start | bytes 245768 | tf_op jit(solution)/shard_map/ppermute | solution.py:15
  24.9 10.2 %collective-permute-start.7 = (bf16[20,16,128]{2,1,0:T(8,128)(2,1)S(1)}, bf16[20,16,128]{2,1,0:T(8,128)(2,1)S(1)}, u32[]{:S(2)}, u32[]{:S(2)}) collective-permute-start(bf16[20,16,128]{2,1,0:T(8,128)(2,1)S(1)} %get-tuple-element.22), channel_id=1, source_target_pairs={{0,7},{1,0},{2,1},{3,2},{4,3},{5,4},{6,5},{7,6},{8,15},{9,8},{10,9... | collective-permute-start | bytes 245768 | tf_op jit(solution)/shard_map/ppermute | solution.py:15
  27.8 7.3 %copy-start.1 = (bf16[3,4,32,16]{2,3,1,0:T(8,128)(2,1)S(1)}, bf16[3,4,32,16]{2,3,1,0:T(8,128)(2,1)}, u32[]{:S(2)}) copy-start(bf16[3,4,32,16]{2,3,1,0:T(8,128)(2,1)} %param.10) | copy-start | bytes 36868
  27.8 7.3 %copy-start.2 = (bf16[8,128,64]{1,2,0:T(8,128)(2,1)S(1)}, bf16[8,128,64]{1,2,0:T(8,128)(2,1)}, u32[]{:S(2)}) copy-start(bf16[8,128,64]{1,2,0:T(8,128)(2,1)} %param.13) | copy-start | bytes 393220
  27.8 7.3 %copy-start.3 = (bf16[9,4,128,128]{3,2,1,0:T(8,128)(2,1)S(1)}, bf16[9,4,128,128]{3,2,1,0:T(8,128)(2,1)}, u32[]{:S(2)}) copy-start(bf16[9,4,128,128]{3,2,1,0:T(8,128)(2,1)} %get-tuple-element.27.wj_ref) | copy-start | bytes 3538948
  27.8 7.3 %copy-start.4 = (bf16[9,3,128,128]{3,2,1,0:T(8,128)(2,1)S(1)}, bf16[9,3,128,128]{3,2,1,0:T(8,128)(2,1)}, u32[]{:S(2)}) copy-start(bf16[9,3,128,128]{3,2,1,0:T(8,128)(2,1)} %get-tuple-element.24.w1_ref) | copy-start | bytes 2654212
  27.8 7.3 %copy-start.5 = (bf16[9,3,128,128]{3,2,1,0:T(8,128)(2,1)S(1)}, bf16[9,3,128,128]{3,2,1,0:T(8,128)(2,1)}, u32[]{:S(2)}) copy-start(bf16[9,3,128,128]{3,2,1,0:T(8,128)(2,1)} %get-tuple-element.25.w2_ref) | copy-start | bytes 2654212
  27.8 7.3 %copy-start.7 = (bf16[1024,128]{1,0:T(8,128)(2,1)S(1)}, bf16[1024,128]{1,0:T(8,128)(2,1)}, u32[]{:S(2)}) copy-start(bf16[1024,128]{1,0:T(8,128)(2,1)} %get-tuple-element.28.wh_ref) | copy-start | bytes 786436
  27.9 7.3 %copy-start.8 = (bf16[128,512]{1,0:T(8,128)(2,1)S(1)}, bf16[128,512]{1,0:T(8,128)(2,1)}, u32[]{:S(2)}) copy-start(bf16[128,512]{1,0:T(8,128)(2,1)} %get-tuple-element.26.wu_ref) | copy-start | bytes 393220

commit v4 on v3

--- a/solution.py
+++ b/solution.py
@@ -397,7 +397,7 @@
         FIELDS + [
             V((14, 3, 2, 4, 2, 16, 128), BF), V((14, 8, 4, 16, 128), BF), V((7, 2, 5, 5, 16, 128), BF),
             V((6, 2, 5, 4, 16, 128), BF), V((5, 2, 3, 2, 16, 128), BF), V((5, 2, 8, 4, 16, 128), BF),
-            V((4, 8, 4, 16, 128), BF), V((4, 8, 4, 16, 128), BF), V((192, 128), F32),
+            V((4, 8, 4, 16, 128), BF), V((4, 8, 4, 16, 128), BF), V((200, 128), F32),
             V((864, 256), F32), pltpu.SemaphoreType.DMA((2,)),
         ], limit=OUTER, flops=16_000_000_000,
     )

time: 56.7 us -> 56.7 us (level)
  no operation moved by 1% of the time
where the time goes in v4:
time: 56.7 us; the launch traced here: 55.7 us
  Pallas kernels  34.3 us (60%)
  starting transfers between devices  17.2 us (30%)
  waiting for transfers between devices  3.01 us (5%)
  local copies, waits for them, and re-layouts  0.83 us (1%)
    pallas_call x6, Pallas kernels, call(): pl.pallas_call(body, out_shape=[jax.ShapeDtypeStruct(*x) for x in shapes]...  34.3 us
    ppermute x8, starting transfers between devices, shift(): lax.ppermute(block, axis, [(i, (i + step) % count) for i in range(count)])  17.2 us
    ppermute x8, waiting for transfers between devices, shift(): lax.ppermute(block, axis, [(i, (i + step) % count) for i in range(count)])  3.01 us
  transfers between devices with their start and end apart: 8, of which 2 were waited for; matrix products, arithmetic and copies ran while one was open for 0% of the time, Pallas kernels for 25%

profile of v4, /device:TPU:2, one launch (start us, length us, event | category | flops | bytes accessed | tf_op | source)
XLA Modules:
  0.0 55.7 jit_solution(17310779912618222863)
XLA Ops:
  0.0 0.8 %copy-done = bf16[3,4,32,16]{2,3,1,0:T(8,128)(2,1)S(1)} copy-done((bf16[3,4,32,16]{2,3,1,0:T(8,128)(2,1)S(1)}, bf16[3,4,32,16]{2,3,1,0:T(8,128)(2,1)}, u32[]{:S(2)}) %copy-start) | copy-done | bytes 12312
  0.8 0.1 shard_map.100
  0.9 3.3 %collective-permute-start = (bf16[4,8,128]{2,1,0:T(8,128)(2,1)S(1)}, bf16[4,8,128]{2,1,0:T(8,128)(2,1)S(1)}, u32[]{:S(2)}, u32[]{:S(2)}) collective-permute-start(bf16[4,8,128]{2,1,0:T(8,128)(2,1)S(1)} %get-tuple-element.18), channel_id=1, source_target_pairs={{0,8},{8,16},{16,24},{24,0},{1,9},{9,17},{17,25},{25,1},{2,10},{10... | collective-permute-start | bytes 24584 | tf_op jit(solution)/shard_map/ppermute | solution.py:15
  4.2 3.1 %collective-permute-start.1 = (bf16[4,8,128]{2,1,0:T(8,128)(2,1)S(1)}, bf16[4,8,128]{2,1,0:T(8,128)(2,1)S(1)}, u32[]{:S(2)}, u32[]{:S(2)}) collective-permute-start(bf16[4,8,128]{2,1,0:T(8,128)(2,1)S(1)} %get-tuple-element.20), channel_id=1, source_target_pairs={{0,24},{8,0},{16,8},{24,16},{1,25},{9,1},{17,9},{25,17},{2,26},{10... | collective-permute-start | bytes 24584 | tf_op jit(solution)/shard_map/ppermute | solution.py:15
  7.4 1.5 %collective-permute-done.before_ref = bf16[4,8,128]{2,1,0:T(8,128)(2,1)S(1)} collective-permute-done((bf16[4,8,128]{2,1,0:T(8,128)(2,1)S(1)}, bf16[4,8,128]{2,1,0:T(8,128)(2,1)S(1)}, u32[]{:S(2)}, u32[]{:S(2)}) %collective-permute-start) | collective-permute-done | bytes 8224 | tf_op jit(solution)/shard_map/ppermute | solution.py:15
  8.9 1.4 %collective-permute-done.1.after_ref = bf16[4,8,128]{2,1,0:T(8,128)(2,1)S(1)} collective-permute-done((bf16[4,8,128]{2,1,0:T(8,128)(2,1)S(1)}, bf16[4,8,128]{2,1,0:T(8,128)(2,1)S(1)}, u32[]{:S(2)}, u32[]{:S(2)}) %collective-permute-start.1) | collective-permute-done | bytes 8224 | tf_op jit(solution)/shard_map/ppermute | solution.py:15
  10.4 2.7 %collective-permute-start.5 = (bf16[4,48,128]{2,1,0:T(8,128)(2,1)S(1)}, bf16[4,48,128]{2,1,0:T(8,128)(2,1)S(1)}, u32[]{:S(2)}, u32[]{:S(2)}) collective-permute-start(bf16[4,48,128]{2,1,0:T(8,128)(2,1)S(1)} %shard_map.101.b2), channel_id=1, source_target_pairs={{0,192},{32,224},{64,0},{96,32},{128,64},{160,96},{192,128},{224,1... | collective-permute-start | bytes 147464 | tf_op jit(solution)/shard_map/ppermute | solution.py:15
  13.0 1.4 %collective-permute-start.4 = (bf16[4,48,128]{2,1,0:T(8,128)(2,1)S(1)}, bf16[4,48,128]{2,1,0:T(8,128)(2,1)S(1)}, u32[]{:S(2)}, u32[]{:S(2)}) collective-permute-start(bf16[4,48,128]{2,1,0:T(8,128)(2,1)S(1)} %shard_map.101.b2), channel_id=1, source_target_pairs={{0,224},{32,0},{64,32},{96,64},{128,96},{160,128},{192,160},{224,1... | collective-permute-start | bytes 147464 | tf_op jit(solution)/shard_map/ppermute | solution.py:15
  14.4 0.6 %collective-permute-start.3 = (bf16[4,48,128]{2,1,0:T(8,128)(2,1)S(1)}, bf16[4,48,128]{2,1,0:T(8,128)(2,1)S(1)}, u32[]{:S(2)}, u32[]{:S(2)}) collective-permute-start(bf16[4,48,128]{2,1,0:T(8,128)(2,1)S(1)} %shard_map.101.b2), channel_id=1, source_target_pairs={{0,32},{32,64},{64,96},{96,128},{128,160},{160,192},{192,224},{224... | collective-permute-start | bytes 147464 | tf_op jit(solution)/shard_map/ppermute | solution.py:15
  15.0 3.1 %collective-permute-start.2 = (bf16[4,48,128]{2,1,0:T(8,128)(2,1)S(1)}, bf16[4,48,128]{2,1,0:T(8,128)(2,1)S(1)}, u32[]{:S(2)}, u32[]{:S(2)}) collective-permute-start(bf16[4,48,128]{2,1,0:T(8,128)(2,1)S(1)} %shard_map.101.b2), channel_id=1, source_target_pairs={{0,64},{32,96},{64,128},{96,160},{128,192},{160,224},{192,0},{224,... | collective-permute-start | bytes 147464 | tf_op jit(solution)/shard_map/ppermute | solution.py:15
  18.1 6.5 %shard_map.103 = (bf16[2816,128]{1,0:T(8,128)(2,1)}, bf16[9,3,128,128]{3,2,1,0:T(8,128)(2,1)}, bf16[9,3,128,128]{3,2,1,0:T(8,128)(2,1)}, bf16[128,512]{1,0:T(8,1...) custom-call(bf16[3,27,64]{2,1,0:T(8,128)(2,1)} %bitcast.9, bf16[3,64]{1,0:T(4,128)(2,1)} %h_ref.1, ...), custom_call_target="tpu_custom_call" | custom-call | flops 6000000000 | bytes 2000000 | tf_op jit(solution)/shard_map/pallas_call | solution.py:360
  24.6 0.0 copy-start.6
  24.6 0.0 collective-permute-done.5.b4
  24.7 0.0 collective-permute-done.4.b3
  24.7 0.0 collective-permute-done.3.b1
  24.7 0.0 collective-permute-done.2.b0
  24.7 0.2 shard_map.102
  24.8 0.0 collective-permute-start.6
  24.9 2.9 %collective-permute-start.7 = (bf16[20,16,128]{2,1,0:T(8,128)(2,1)S(1)}, bf16[20,16,128]{2,1,0:T(8,128)(2,1)S(1)}, u32[]{:S(2)}, u32[]{:S(2)}) collective-permute-start(bf16[20,16,128]{2,1,0:T(8,128)(2,1)S(1)} %get-tuple-element.22), channel_id=1, source_target_pairs={{0,7},{1,0},{2,1},{3,2},{4,3},{5,4},{6,5},{7,6},{8,15},{9,8},{10,9... | collective-permute-start | bytes 245768 | tf_op jit(solution)/shard_map/ppermute | solution.py:15
  27.8 0.0 copy-done.6
  27.8 0.0 copy-start.4
  27.8 0.0 copy-start.5
  27.8 0.0 copy-start.7
  27.9 0.0 copy-start.8
  27.9 7.2 %shard_map.104 = (bf16[6,3,2,4,2,16,128]{6,5,4,3,2,1,0:T(8,128)(2,1)S(1)}, bf16[6,8,4,16,128]{4,3,2,1,0:T(8,128)(2,1)S(1)}) custom-call(bf16[4,48,128]{2,1,0:T(8,128)(2,1)S(1)} %collective-permute-done.2.b0, bf16[4,48,128]{2,1,0:T(8,128)(2,1)S(1)} %collective-permute-done.3.b1, bf16[4,48,128]{2,1,0:T(8,128)(2,1)S(1)} %shard_map.101.b2, ...), custom_call_target="tpu_custom_call" | custom-call | flops 8000000000 | bytes 2000000 | tf_op jit(solution)/shard_map/pallas_call | solution.py:360
  35.1 0.0 collective-permute-done.6.left_ref
  35.1 0.0 collective-permute-done.7.right_ref
  35.1 0.0 copy-done.1
  35.1 0.0 copy-done.2
  35.1 0.0 copy-done.3
  35.1 0.0 copy-done.4
  35.2 20.4 %shard_map.105 = f32[3,4,16,32]{3,2,1,0:T(8,128)} custom-call(bf16[4,48,128]{2,1,0:T(8,128)(2,1)S(1)} %collective-permute-done.2.b0, bf16[4,48,128]{2,1,0:T(8,128)(2,1)S(1)} %collective-permute-done.3.b1, bf16[4,48,128]{2,1,0:T(8,128)(2,1)S(1)} %shard_map.101.b2, bf16[4,48,128]{2,1,0:T(8,128)(2,1)S(1)} %collective-permute-done.4.b3, ...), custom_call_target="tpu_custom_call" | custom-call | flops 16000000000 | bytes 2000000 | tf_op jit(solution)/shard_map/pallas_call | solution.py:360
  (8 shorter events, 0.0 us)
Async XLA Ops:
  0.0 0.8 %copy-start = (bf16[3,4,32,16]{2,3,1,0:T(8,128)(2,1)S(1)}, bf16[3,4,32,16]{2,3,1,0:T(8,128)(2,1)}, u32[]{:S(2)}) copy-start(bf16[3,4,32,16]{2,3,1,0:T(8,128)(2,1)} %param.10) | copy-start | bytes 36868
  0.9 8.0 %collective-permute-start = (bf16[4,8,128]{2,1,0:T(8,128)(2,1)S(1)}, bf16[4,8,128]{2,1,0:T(8,128)(2,1)S(1)}, u32[]{:S(2)}, u32[]{:S(2)}) collective-permute-start(bf16[4,8,128]{2,1,0:T(8,128)(2,1)S(1)} %get-tuple-element.18), channel_id=1, source_target_pairs={{0,8},{8,16},{16,24},{24,0},{1,9},{9,17},{17,25},{25,1},{2,10},{10... | collective-permute-start | bytes 24584 | tf_op jit(solution)/shard_map/ppermute | solution.py:15
  4.2 6.1 %collective-permute-start.1 = (bf16[4,8,128]{2,1,0:T(8,128)(2,1)S(1)}, bf16[4,8,128]{2,1,0:T(8,128)(2,1)S(1)}, u32[]{:S(2)}, u32[]{:S(2)}) collective-permute-start(bf16[4,8,128]{2,1,0:T(8,128)(2,1)S(1)} %get-tuple-element.20), channel_id=1, source_target_pairs={{0,24},{8,0},{16,8},{24,16},{1,25},{9,1},{17,9},{25,17},{2,26},{10... | collective-permute-start | bytes 24584 | tf_op jit(solution)/shard_map/ppermute | solution.py:15
  10.4 14.3 %collective-permute-start.5 = (bf16[4,48,128]{2,1,0:T(8,128)(2,1)S(1)}, bf16[4,48,128]{2,1,0:T(8,128)(2,1)S(1)}, u32[]{:S(2)}, u32[]{:S(2)}) collective-permute-start(bf16[4,48,128]{2,1,0:T(8,128)(2,1)S(1)} %shard_map.101.b2), channel_id=1, source_target_pairs={{0,192},{32,224},{64,0},{96,32},{128,64},{160,96},{192,128},{224,1... | collective-permute-start | bytes 147464 | tf_op jit(solution)/shard_map/ppermute | solution.py:15
  13.0 11.6 %collective-permute-start.4 = (bf16[4,48,128]{2,1,0:T(8,128)(2,1)S(1)}, bf16[4,48,128]{2,1,0:T(8,128)(2,1)S(1)}, u32[]{:S(2)}, u32[]{:S(2)}) collective-permute-start(bf16[4,48,128]{2,1,0:T(8,128)(2,1)S(1)} %shard_map.101.b2), channel_id=1, source_target_pairs={{0,224},{32,0},{64,32},{96,64},{128,96},{160,128},{192,160},{224,1... | collective-permute-start | bytes 147464 | tf_op jit(solution)/shard_map/ppermute | solution.py:15
  14.4 10.2 %collective-permute-start.3 = (bf16[4,48,128]{2,1,0:T(8,128)(2,1)S(1)}, bf16[4,48,128]{2,1,0:T(8,128)(2,1)S(1)}, u32[]{:S(2)}, u32[]{:S(2)}) collective-permute-start(bf16[4,48,128]{2,1,0:T(8,128)(2,1)S(1)} %shard_map.101.b2), channel_id=1, source_target_pairs={{0,32},{32,64},{64,96},{96,128},{128,160},{160,192},{192,224},{224... | collective-permute-start | bytes 147464 | tf_op jit(solution)/shard_map/ppermute | solution.py:15
  15.0 9.6 %collective-permute-start.2 = (bf16[4,48,128]{2,1,0:T(8,128)(2,1)S(1)}, bf16[4,48,128]{2,1,0:T(8,128)(2,1)S(1)}, u32[]{:S(2)}, u32[]{:S(2)}) collective-permute-start(bf16[4,48,128]{2,1,0:T(8,128)(2,1)S(1)} %shard_map.101.b2), channel_id=1, source_target_pairs={{0,64},{32,96},{64,128},{96,160},{128,192},{160,224},{192,0},{224,... | collective-permute-start | bytes 147464 | tf_op jit(solution)/shard_map/ppermute | solution.py:15
  24.6 3.2 %copy-start.6 = (bf16[2816,128]{1,0:T(8,128)(2,1)S(1)}, bf16[2816,128]{1,0:T(8,128)(2,1)}, u32[]{:S(2)}) copy-start(bf16[2816,128]{1,0:T(8,128)(2,1)} %get-tuple-element.23.wb_ref) | copy-start | bytes 2162692
  24.8 10.2 %collective-permute-start.6 = (bf16[20,16,128]{2,1,0:T(8,128)(2,1)S(1)}, bf16[20,16,128]{2,1,0:T(8,128)(2,1)S(1)}, u32[]{:S(2)}, u32[]{:S(2)}) collective-permute-start(bf16[20,16,128]{2,1,0:T(8,128)(2,1)S(1)} %get-tuple-element.21), channel_id=1, source_target_pairs={{0,1},{1,2},{2,3},{3,4},{4,5},{5,6},{6,7},{7,0},{8,9},{9,10},{10,1... | collective-permute-start | bytes 245768 | tf_op jit(solution)/shard_map/ppermute | solution.py:15
  24.9 10.2 %collective-permute-start.7 = (bf16[20,16,128]{2,1,0:T(8,128)(2,1)S(1)}, bf16[20,16,128]{2,1,0:T(8,128)(2,1)S(1)}, u32[]{:S(2)}, u32[]{:S(2)}) collective-permute-start(bf16[20,16,128]{2,1,0:T(8,128)(2,1)S(1)} %get-tuple-element.22), channel_id=1, source_target_pairs={{0,7},{1,0},{2,1},{3,2},{4,3},{5,4},{6,5},{7,6},{8,15},{9,8},{10,9... | collective-permute-start | bytes 245768 | tf_op jit(solution)/shard_map/ppermute | solution.py:15
  27.8 7.3 %copy-start.1 = (bf16[3,4,32,16]{2,3,1,0:T(8,128)(2,1)S(1)}, bf16[3,4,32,16]{2,3,1,0:T(8,128)(2,1)}, u32[]{:S(2)}) copy-start(bf16[3,4,32,16]{2,3,1,0:T(8,128)(2,1)} %param.10) | copy-start | bytes 36868
  27.8 7.3 %copy-start.2 = (bf16[8,128,64]{1,2,0:T(8,128)(2,1)S(1)}, bf16[8,128,64]{1,2,0:T(8,128)(2,1)}, u32[]{:S(2)}) copy-start(bf16[8,128,64]{1,2,0:T(8,128)(2,1)} %param.13) | copy-start | bytes 393220
  27.8 7.3 %copy-start.3 = (bf16[9,4,128,128]{3,2,1,0:T(8,128)(2,1)S(1)}, bf16[9,4,128,128]{3,2,1,0:T(8,128)(2,1)}, u32[]{:S(2)}) copy-start(bf16[9,4,128,128]{3,2,1,0:T(8,128)(2,1)} %get-tuple-element.27.wj_ref) | copy-start | bytes 3538948
  27.8 7.3 %copy-start.4 = (bf16[9,3,128,128]{3,2,1,0:T(8,128)(2,1)S(1)}, bf16[9,3,128,128]{3,2,1,0:T(8,128)(2,1)}, u32[]{:S(2)}) copy-start(bf16[9,3,128,128]{3,2,1,0:T(8,128)(2,1)} %get-tuple-element.24.w1_ref) | copy-start | bytes 2654212
  27.8 7.3 %copy-start.5 = (bf16[9,3,128,128]{3,2,1,0:T(8,128)(2,1)S(1)}, bf16[9,3,128,128]{3,2,1,0:T(8,128)(2,1)}, u32[]{:S(2)}) copy-start(bf16[9,3,128,128]{3,2,1,0:T(8,128)(2,1)} %get-tuple-element.25.w2_ref) | copy-start | bytes 2654212
  27.8 7.3 %copy-start.7 = (bf16[1024,128]{1,0:T(8,128)(2,1)S(1)}, bf16[1024,128]{1,0:T(8,128)(2,1)}, u32[]{:S(2)}) copy-start(bf16[1024,128]{1,0:T(8,128)(2,1)} %get-tuple-element.28.wh_ref) | copy-start | bytes 786436
  27.9 7.3 %copy-start.8 = (bf16[128,512]{1,0:T(8,128)(2,1)S(1)}, bf16[128,512]{1,0:T(8,128)(2,1)}, u32[]{:S(2)}) copy-start(bf16[128,512]{1,0:T(8,128)(2,1)} %get-tuple-element.26.wu_ref) | copy-start | bytes 393220
